TPU v7x, 32 devices: a whole 2x2x4 slice. The times are simulated.
32 devices in a mesh: row: 4 (over y, x), col: 8 (over z, core).
Axes of the slice: x: 2, y: 2, z: 4, core: 2. Of those that a mesh axis runs over, the one named last changes fastest.
Arguments:
- covariance: float32 [16384, 16384], P('row', 'col'), may hold values from -1 to 560
- seed_index: int32 [128], replicated, may hold values from 0 to 16383, as said below
Outputs:
- basis: float32 [16384, 384], P('row')
- projection: float32 [384, 256], replicated
- first_pass: float32 [384, 256], replicated
Inputs may be any that keep to these rules, and one draw needn't show every extreme that they name: `seed_index`: 128 distinct column indices.
All inputs are finite; a program needn't handle non-finite values.
Results may differ from a plain program's by a relative error of at most 0.00019.
Values sent between devices are 32-bit elements; how exact they have to be, the bound alone decides.
A program may use at most 128 MiB of HBM per device.

v0:
```python
import jax
import jax.numpy as jnp
from jax import lax
from jax.sharding import PartitionSpec as P

N = 16384
ITERS = 2


def product(left, right):
    return jnp.dot(left, right, precision=lax.Precision.HIGH, preferred_element_type=jnp.float32)


def small_sum(value, axis):
    return jnp.sum(lax.all_gather(value, axis, axis=0), axis=0)


def finish_block(block, gram):
    lower = jnp.linalg.cholesky(gram)
    basis_block = jax.scipy.linalg.solve_triangular(lower, block.T, lower=True).T
    return (basis_block, lower.T)


def to_row_layout(piece, rows, cols):
    perm = [(r * cols + c, c * rows + r) for r in range(rows) for c in range(cols)]
    moved = lax.ppermute(piece, ("row", "col"), perm)
    return lax.all_gather(moved, "col", axis=0, tiled=True)


def solve(rows, cols, covariance, seed_index):
    row_count, col_count = covariance.shape
    width = seed_index.shape[0]
    row_place = lax.axis_index("row")
    piece_count = col_count // rows
    offsets = seed_index - row_place * row_count
    inside = (offsets >= 0) & (offsets < row_count)
    picked = jnp.take(covariance, jnp.clip(offsets, 0, row_count - 1), axis=0)
    start = lax.psum(jnp.where(inside[:, None], picked, 0.0), "row").T
    gram = small_sum(product(start.T, start), "col")
    vector, upper = finish_block(start, gram)
    piece = lax.dynamic_slice_in_dim(vector, row_place * piece_count, piece_count, 0)
    current = to_row_layout(piece, rows, cols)
    blocks = [current]
    projection = jnp.zeros(((ITERS + 1) * width, ITERS * width), jnp.float32)
    first_pass = jnp.zeros(((ITERS + 1) * width, ITERS * width), jnp.float32)
    for section in range(ITERS):
        stacked = jnp.concatenate(blocks, axis=1)
        if section == 0:
            image = lax.psum(product(covariance, vector), "col")
        else:
            partial_value = product(current.T, covariance).T
            piece = lax.psum_scatter(partial_value, "row", scatter_dimension=0, tiled=True)
            image = to_row_layout(piece, rows, cols)
        first = small_sum(product(stacked.T, image), "row")
        once = image - product(stacked, first)
        both = product(jnp.concatenate([stacked, once], axis=1).T, once)
        both = small_sum(both, "row")
        second, raw_gram = both[: (section + 1) * width], both[(section + 1) * width :]
        twice = once - product(stacked, second)
        gram = raw_gram - product(second.T, second)
        current, upper = finish_block(twice, gram)
        projection = projection.at[
            : (section + 1) * width, section * width : (section + 1) * width
        ].set(first + second)
        projection = projection.at[
            (section + 1) * width : (section + 2) * width, section * width : (section + 1) * width
        ].set(upper)
        first_pass = first_pass.at[
            : (section + 1) * width, section * width : (section + 1) * width
        ].set(first)
        blocks.append(current)
    basis = jnp.concatenate(blocks, axis=1) * jnp.float32(N**0.5)
    return (basis, projection, first_pass)


def solution(mesh):
    rows, cols = mesh.shape["row"], mesh.shape["col"]
    return jax.shard_map(
        lambda covariance, seed_index: solve(rows, cols, covariance, seed_index),
        mesh=mesh,
        in_specs=(P("row", "col"), P()),
        out_specs=(P("row", None), P(), P()),
        check_vma=False,
    )
```

profile of v0, /device:TPU:0, one launch (start us, length us, event | category | flops | bytes accessed | tf_op | source)
XLA Modules:
  0.0 473.1 jit_solution(1931504965210466814)
XLA Ops:
  7.2 0.7 compare_and_fusion
  7.9 12.0 %gather_fusion = f32[128,2048]{1,0:T(8,128)S(1)} fusion(f32[4096,2048]{1,0:T(8,128)} %param.17, s32[1024]{0:T(1024)S(1)} %pad_clamp_fusion), kind=kCustom, calls=%fused_computation | custom fusion | bytes 2097664 | tf_op jit(solution)/shard_map/jit(_take)/gather | solution.py:37
  19.9 1.2 select_select_fusion
  21.1 0.0 all-reduce.7.cloned.1.call-start
  21.1 55.3 %all-reduce.5.cloned.1.call-done = f32[128,2048]{1,0:T(8,128)} async-done(((f32[128,2048]{1,0:T(8,128)}), f32[128,2048]{1,0:T(8,128)}) %all-reduce.5.cloned.1.call-update) | async-done | bytes 1048592 | tf_op jit(solution)/shard_map/psum | solution.py:38
  76.4 2.2 fusion.30
  78.7 14.8 %all-gather = f32[1024,128]{1,0:T(8,128)S(1)} all-gather(f32[128,128]{1,0:T(8,128)S(1)} %fusion.30), channel_id=2, replica_groups=mesh['row'=4,'col'=8] {'col'}, dimensions={0}, use_global_device_ids=true | all-gather | bytes 589824 | tf_op jit(solution)/shard_map/all_gather | solution.py:15
  93.4 0.1 copy.13
  93.6 11.7 %cholesky.59 = f32[128,128]{1,0:T(8,128)S(1)} custom-call(f32[128,128]{1,0:T(8,128)S(1)} %fusion.19), custom_call_target="Cholesky" | custom-call | tf_op jit(solution)/shard_map/jit(cholesky)/cholesky | solution.py:19
  105.3 0.6 compare_reduce_fusion.2
  106.0 0.7 fusion.11
  106.6 9.8 %custom-call.9 = f32[1,128,128]{1,2,0:T(8,128)S(1)} custom-call(f32[1,128,128]{2,1,0:T(8,128)S(1)} %fusion.11), custom_call_target="InvertDiagBlocksLowerTriangular" | custom-call | tf_op jit(solution)/shard_map/jit(_solve_triangular)/triangular_solve | solution.py:20
  116.4 1.1 fusion.17
  117.5 24.0 %convolution_bitcast_fusion.1 = f32[4096,128]{0,1:T(8,128)} fusion(f32[128,2048]{1,0:T(8,128)S(1)} %fusion.17, f32[4096,2048]{1,0:T(8,128)} %param.17), kind=kOutput, calls=%fused_computation.15 | convolution fusion | flops 6442450944 | bytes 36700160 | tf_op jit(solution)/shard_map/dot_general | solution.py:11
  141.6 0.0 all-gather.8.cloned.1.call-start
  141.6 0.7 collective-permute-start
  142.3 0.7 copy-done.10
  143.1 0.0 reduce-scatter.2.cloned.1.call-start
  143.1 69.0 %all-reduce.7.cloned.1.call-done = f32[4096,128]{0,1:T(8,128)} async-done(((f32[4096,128]{0,1:T(8,128)}), f32[4096,128]{0,1:T(8,128)}) %all-reduce.7.cloned.1.call-update) | async-done | bytes 2097168 | tf_op jit(solution)/shard_map/psum | solution.py:49
  212.1 31.0 %all-gather.8.cloned.1.call-done = f32[4096,128]{0,1:T(8,128)} async-done(((f32[512,128]{0,1:T(8,128)}), f32[4096,128]{0,1:T(8,128)}) %all-gather.8.cloned.1.call-update) | async-done | bytes 2097168 | tf_op jit(solution)/shard_map/all_gather | solution.py:27
  243.1 3.4 fusion.31
  246.5 8.9 %all-gather.1 = f32[512,128]{1,0:T(8,128)S(1)} all-gather(f32[128,128]{1,0:T(8,128)S(1)} %fusion.31), channel_id=3, replica_groups=mesh['row'=4,'col'=8] {'row'}, dimensions={0}, use_global_device_ids=true | all-gather | bytes 327680 | tf_op jit(solution)/shard_map/all_gather | solution.py:15
  255.4 2.7 convolution_subtract_fusion.3
  258.1 1.9 fusion.5
  260.1 11.0 %all-gather.2 = f32[1024,128]{1,0:T(8,128)S(1)} all-gather(f32[256,128]{1,0:T(8,128)S(1)} %fusion.5), channel_id=4, replica_groups=mesh['row'=4,'col'=8] {'row'}, dimensions={0}, use_global_device_ids=true | all-gather | bytes 655360 | tf_op jit(solution)/shard_map/all_gather | solution.py:15
  271.1 0.1 copy.25
  271.2 0.3 convolution_subtract_fusion.5
  271.4 0.1 copy.16
  271.6 11.7 %cholesky.70 = f32[128,128]{1,0:T(8,128)S(1)} custom-call(f32[128,128]{1,0:T(8,128)S(1)} %fusion.16), custom_call_target="Cholesky" | custom-call | tf_op jit(solution)/shard_map/jit(cholesky)/cholesky | solution.py:19
  283.3 0.6 compare_reduce_fusion.1
  283.9 0.7 fusion.22
  284.6 9.8 %custom-call.11 = f32[1,128,128]{1,2,0:T(8,128)S(1)} custom-call(f32[1,128,128]{2,1,0:T(8,128)S(1)} %get-tuple-element.92), custom_call_target="InvertDiagBlocksLowerTriangular" | custom-call | tf_op jit(solution)/shard_map/jit(_solve_triangular)/triangular_solve | solution.py:20
  294.4 2.7 fusion.4
  297.1 3.3 fusion.14
  300.4 15.8 %convolution_bitcast_fusion.2 = f32[2048,128]{0,1:T(8,128)} fusion(f32[128,4096]{1,0:T(8,128)} %fusion.14, f32[4096,2048]{1,0:T(8,128)} %param.17), kind=kOutput, calls=%fused_computation.19 | convolution fusion | flops 6442450944 | bytes 36700160 | tf_op jit(solution)/shard_map/dot_general | solution.py:11
  316.2 0.0 all-gather.10.cloned.1.call-start
  316.2 26.5 %reduce-scatter.2.cloned.1.call-done = f32[512,128]{0,1:T(8,128)} async-done(((f32[2048,128]{0,1:T(8,128)}), f32[512,128]{0,1:T(8,128)}) %reduce-scatter.2.cloned.1.call-update) | async-done | bytes 262160 | tf_op jit(solution)/shard_map/reduce_scatter | solution.py:52
  342.7 1.7 collective-permute-start.1
  344.5 0.7 copy-done.9
  345.3 0.7 and_reduce_fusion
  346.0 0.6 fusion.29
  346.6 0.8 scatter.26
  347.4 0.1 copy.20
  347.5 39.0 %all-gather.10.cloned.1.call-done = f32[4096,128]{0,1:T(8,128)} async-done(((f32[512,128]{0,1:T(8,128)}), f32[4096,128]{0,1:T(8,128)}) %all-gather.10.cloned.1.call-update) | async-done | bytes 2097168 | tf_op jit(solution)/shard_map/all_gather | solution.py:27
  386.5 4.0 fusion.7
  390.5 10.0 %all-gather.3 = f32[1024,128]{1,0:T(8,128)S(1)} all-gather(f32[256,128]{1,0:T(8,128)S(1)} %fusion.7), channel_id=5, replica_groups=mesh['row'=4,'col'=8] {'row'}, dimensions={0}, use_global_device_ids=true | all-gather | bytes 655360 | tf_op jit(solution)/shard_map/all_gather | solution.py:15
  400.6 3.7 convolution_subtract_fusion.1
  404.3 2.7 fusion
  407.0 12.1 %all-gather.4 = f32[1536,128]{1,0:T(8,128)S(1)} all-gather(f32[384,128]{1,0:T(8,128)S(1)} %fusion), channel_id=6, replica_groups=mesh['row'=4,'col'=8] {'row'}, dimensions={0}, use_global_device_ids=true | all-gather | bytes 983040 | tf_op jit(solution)/shard_map/all_gather | solution.py:15
  419.2 0.1 copy.26
  419.3 0.3 convolution_subtract_fusion.4
  419.6 0.1 copy.19
  419.7 11.7 %cholesky.81 = f32[128,128]{1,0:T(8,128)S(1)} custom-call(f32[128,128]{1,0:T(8,128)S(1)} %fusion.13), custom_call_target="Cholesky" | custom-call | tf_op jit(solution)/shard_map/jit(cholesky)/cholesky | solution.py:19
  431.4 0.6 compare_reduce_fusion
  432.1 0.6 fusion.23
  432.7 9.8 %custom-call.12 = f32[1,128,128]{1,2,0:T(8,128)S(1)} custom-call(f32[1,128,128]{2,1,0:T(8,128)S(1)} %get-tuple-element.90), custom_call_target="InvertDiagBlocksLowerTriangular" | custom-call | tf_op jit(solution)/shard_map/jit(_solve_triangular)/triangular_solve | solution.py:20
  442.5 3.6 fusion.3
  446.2 1.9 convolution_bitcast_fusion
  448.1 3.0 maximum_multiply_fusion
  451.1 6.6 %copy.22 = f32[4096,384]{1,0:T(8,128)} copy(f32[4096,384]{0,1:T(8,128)} %maximum_multiply_fusion) | data formatting | bytes 12582912
  457.7 2.0 fusion.8
  459.7 2.8 scatter.24
  462.5 0.1 copy.21
  462.6 3.7 scatter.29
  (47 shorter events, 0.6 us)
Async XLA Ops:
  7.2 69.3 %all-reduce.5.cloned.1.call-start = ((), (), s32[]{:S(2)}) async-start(), calls=%async_computation.1 | async-start | bytes 2097152 | tf_op jit(solution)/shard_map/psum | solution.py:38
  21.1 191.0 %all-reduce.7.cloned.1.call-start = ((), (), s32[]{:S(2)}) async-start(), calls=%async_computation.3 | async-start | bytes 4194304 | tf_op jit(solution)/shard_map/psum | solution.py:49
  76.4 40.0 %copy-start.4 = (f32[128,2048]{1,0:T(8,128)S(1)}, f32[128,2048]{1,0:T(8,128)}, u32[]{:S(2)}) copy-start(f32[128,2048]{1,0:T(8,128)} %all-reduce.5.cloned.1.call-done) | copy-start | bytes 3145732
  141.6 101.5 %all-gather.8.cloned.1.call-start = ((), (), s32[]{:S(2)}) async-start(), calls=%async_computation.2 | async-start | bytes 2359296 | tf_op jit(solution)/shard_map/all_gather | solution.py:27
  141.6 0.7 collective-permute-start
  142.3 0.7 copy-start.10
  143.1 199.7 %reduce-scatter.2.cloned.1.call-start = ((), (), s32[]{:S(2)}) async-start(), calls=%async_computation.4 | async-start | bytes 1310720 | tf_op jit(solution)/shard_map/reduce_scatter | solution.py:52
  243.1 12.4 %copy-start = (f32[4096,128]{0,1:T(8,128)S(1)}, f32[4096,128]{0,1:T(8,128)}, u32[]{:S(2)}) copy-start(f32[4096,128]{0,1:T(8,128)} %all-gather.8.cloned.1.call-done) | copy-start | bytes 6291460
  258.1 1.9 copy-start.3
  316.2 70.3 %all-gather.10.cloned.1.call-start = ((), (), s32[]{:S(2)}) async-start(), calls=%async_computation.5 | async-start | bytes 2359296 | tf_op jit(solution)/shard_map/all_gather | solution.py:27
  342.7 1.8 collective-permute-start.1
  344.5 0.7 copy-start.9
  347.5 39.0 %copy-start.6 = (f32[384,256]{1,0:T(8,128)}, f32[384,256]{1,0:T(8,128)S(1)}, u32[]{:S(2)}) copy-start(f32[384,256]{1,0:T(8,128)S(1)} %constant_dynamic-update-slice_fusion.1) | copy-start | bytes 1179652
  400.6 3.7 copy-start.1
  404.3 2.7 copy-start.5
  446.1 2.0 copy-start.2
  451.1 6.6 %copy-start.7 = (f32[384,256]{1,0:T(8,128)S(1)}, f32[384,256]{1,0:T(8,128)}, u32[]{:S(2)}) copy-start(f32[384,256]{1,0:T(8,128)} %copy-done.6) | copy-start | bytes 1179652
  462.6 3.8 copy-start.8
Sparse Core Ops, SparseCore 0:
  21.2 55.1 all-reduce.4
  141.7 70.3 all-reduce.6
  214.3 28.7 all-gather.7
  316.3 26.4 reduce-scatter.1
  345.4 41.0 all-gather.9
where the time goes:
time: 481 us; the launch traced here: 473 us
  waiting for transfers between devices  221 us (46%)
  other arithmetic  76.3 us (16%)
  matrix products  73.5 us (15%)
  blocking collectives  56.8 us (12%)
  local copies, waits for them, and re-layouts  28.7 us (6%)
  between operations  14.4 us (3%)
    all_gather x2, waiting for transfers between devices, to_row_layout(): return lax.all_gather(moved, 'col', axis=0, tiled=True)  70 us
    psum x1, waiting for transfers between devices, solve(): image = lax.psum(product(covariance, vector), 'col')  69 us
    dot_general x13, matrix products, product(): jnp.dot(left, right, precision=lax.Precision.HIGH, preferred_element_type...  67.3 us
    all_gather x5, blocking collectives, small_sum(): return jnp.sum(lax.all_gather(value, axis, axis=0), axis=0)  56.8 us
    psum x1, waiting for transfers between devices, solve(): start = lax.psum(jnp.where(inside[:, None], picked, 0.0), 'row').T  55.3 us
    another operation x9, other arithmetic, finish_block(): lower = jnp.linalg.cholesky(gram)  37.2 us
    another operation x4, other arithmetic, finish_block(): jax.scipy.linalg.solve_triangular(lower, block.T, lower=True)  30.1 us
    reduce_scatter x1, waiting for transfers between devices, solve(): lax.psum_scatter(partial_value, 'row', scatter_dimension=0, tiled=True)  26.5 us
  transfers between devices with their start and end apart: 7, of which 5 were waited for; matrix products, arithmetic and copies ran while one was open for 0% of the time, Pallas kernels for 0%

commit v1 on v0

v1 whole, which is shorter than its diff:
```python
import functools

import jax
import jax.numpy as jnp
from jax import lax
from jax.experimental import pallas as pl
from jax.experimental.pallas import tpu as pltpu
from jax.sharding import PartitionSpec as P

MESH = pl.DeviceIdType.MESH
F32, BF16 = jnp.float32, jnp.bfloat16
ITERS = 2
LIMIT = 66 * 1024 * 1024 - 2 * 1024 * 1024

NN = (((1,), (0,)), ((), ()))
NT = (((1,), (1,)), ((), ()))
TN = (((0,), (0,)), ((), ()))


def dot(left, right, dims):
    return lax.dot_general(left, right, dims, precision=lax.Precision.HIGHEST, preferred_element_type=F32)


def halves(value):
    high = value.astype(BF16)
    return high, (value - high.astype(F32)).astype(BF16)


def dot3(left, right, dims):
    lh, ll = halves(left)
    rh, rl = halves(right)
    go = functools.partial(lax.dot_general, dimension_numbers=dims, preferred_element_type=F32)
    return go(lh, rh) + (go(lh, rl) + go(ll, rh))


def gather_kernel(rows, index_ref, inside_ref, cov_ref, out_ref, buf, sem):
    width, cols = buf.shape
    wide = cols // rows

    def fetch(i, carry):
        pltpu.make_async_copy(cov_ref.at[pl.ds(index_ref[i], 1), :], buf.at[pl.ds(i, 1), :], sem).start()
        return carry

    lax.fori_loop(0, width, fetch, 0, unroll=8)
    pltpu.make_async_copy(cov_ref.at[pl.ds(0, width), :], buf, sem).wait()
    keep = inside_ref[...] > 0
    for n in range(rows):
        out_ref[n] = jnp.where(keep, buf[:, n * wide : (n + 1) * wide], 0.0)


def gather(rows, covariance, seed_index):
    row_count, cols = covariance.shape
    width = seed_index.shape[0]
    offsets = seed_index - lax.axis_index("row") * row_count
    inside = (offsets >= 0) & (offsets < row_count)
    return pl.pallas_call(
        functools.partial(gather_kernel, rows),
        out_shape=jax.ShapeDtypeStruct((rows, width, cols // rows), F32),
        in_specs=[
            pl.BlockSpec(memory_space=pltpu.SMEM),
            pl.BlockSpec(memory_space=pltpu.VMEM),
            pl.BlockSpec(memory_space=pl.ANY),
        ],
        out_specs=pl.BlockSpec(memory_space=pltpu.VMEM),
        scratch_shapes=[pltpu.VMEM((width, cols), F32), pltpu.SemaphoreType.DMA],
        compiler_params=pltpu.CompilerParams(vmem_limit_bytes=8 * 1024 * 1024),
        name="gather",
    )(jnp.clip(offsets, 0, row_count - 1), inside.astype(jnp.int32)[:, None], covariance)


def factor(gram, work):
    width = gram.shape[0]
    down = lax.broadcasted_iota(jnp.int32, (width, width), 0)
    across = lax.broadcasted_iota(jnp.int32, (width, width), 1)
    work[:, :width] = gram
    work[:, width:] = jnp.where(down == across, 1.0, 0.0)
    lane = lax.broadcasted_iota(jnp.int32, (1, width), 1)
    tall = lax.broadcasted_iota(jnp.int32, (width, 1), 0)

    def step(j, carry):
        row = work[pl.ds(j, 1), :]
        pivot = jnp.sum(jnp.where(lane == j, row[:, :width], 0.0), axis=1, keepdims=True)
        now = work[...]
        column = jnp.sum(jnp.where(across == j, now[:, :width], 0.0), axis=1, keepdims=True)
        scale = lax.rsqrt(pivot)
        scale = scale * (1.5 - 0.5 * pivot * scale * scale)
        unit = row * scale
        ratio = jnp.where(tall > j, column * scale, 0.0)
        work[...] = jnp.where(tall == j, unit, now - ratio * unit)
        return carry

    lax.fori_loop(0, width, step, 0)
    upper = jnp.where(down <= across, work[:, :width], 0.0)
    return upper, work[:, width:]


def main_kernel(
    rows, cols, x_ref, cov_ref,
    wide_ref, small_ref,
    ahi, alo, stage, stage_sem, part, rsbuf, rs_send, rs_recv,
    zbuf, up_send, up_recv, dn_send, dn_recv, rowbuf, pl_send, pl_recv, dd_send, dd_recv, own_sem, out_sem,
    a_loc, a_in, a_z, a_full, a_s1, a_r1, a_s2, a_r2, a_s3, a_r3, work,
):
    zs = cols // 2
    width, wide = x_ref.shape[1], x_ref.shape[2]
    row = lax.axis_index("row")
    col = lax.axis_index("col")
    z = col // 2
    core = col % 2
    plane = 2 * rows
    q = row * 2 + core

    barrier = pltpu.get_barrier_semaphore()
    for d in range(1, plane):
        t = lax.rem(q + d, plane)
        pl.semaphore_signal(barrier, inc=1, device_id=(t // 2, 2 * z + t % 2), device_id_type=MESH)
    for d in range(1, zs):
        t = lax.rem(z + d, zs)
        pl.semaphore_signal(barrier, inc=1, device_id=(row, 2 * t + core), device_id_type=MESH)
    pl.semaphore_wait(barrier, plane - 1 + zs - 1)

    pending = []

    def send(src, dst, ssem, rsem, dev):
        return pltpu.make_async_remote_copy(
            src_ref=src, dst_ref=dst, send_sem=ssem, recv_sem=rsem, device_id=dev, device_id_type=MESH
        )

    def rs_copies(u, src):
        out = []
        for d in range(1, rows):
            t = lax.rem(row + d, rows)
            out.append(send(src.at[t], rsbuf.at[u, d - 1], rs_send.at[u, d - 1], rs_recv.at[u, d - 1], (t, col)))
        return out

    def rs_start(u, src):
        for copy in rs_copies(u, src):
            copy.start()

    def rs_finish(u, src):
        total = src[row]
        for d, copy in enumerate(rs_copies(u, src)):
            copy.wait_recv()
            total = total + rsbuf[u, d]
        for copy in rs_copies(u, src):
            copy.wait_send()
        return total

    def up_copy(u, s):
        return send(zbuf.at[u, s], zbuf.at[u, s], up_send.at[u, s], up_recv.at[u, s], (row, col + 2))

    def dn_copy(u, s):
        return send(zbuf.at[u, s], zbuf.at[u, s], dn_send.at[u, s], dn_recv.at[u, s], (row, col - 2))

    def plane_copy(u, t, slot, d):
        return send(zbuf.at[u, t], rowbuf.at[u, slot], pl_send.at[u, d], pl_recv.at[u, d], (t, col))

    def slot_of(k, r):
        return k * rows + r

    def to_plane(u, s):
        @pl.when(s != row)
        def _():
            plane_copy(u, s, slot_of(core, row), lax.rem(s - row + rows, rows)).start()

        @pl.when(s == row)
        def _():
            pltpu.make_async_copy(zbuf.at[u, s], rowbuf.at[u, slot_of(core, row)], own_sem.at[u]).start()

    def spread_start(u, piece):
        zbuf[u, z] = piece

        @pl.when(z + 1 < zs)
        def _():
            up_copy(u, z).start()

        @pl.when(z > 0)
        def _():
            dn_copy(u, z).start()

        to_plane(u, z)

    def spread_step(u, s):
        low, high = z - s, z + s

        @pl.when(low >= 0)
        def _():
            up_copy(u, low).wait_recv()

            @pl.when(z + 1 < zs)
            def _():
                up_copy(u, low).start()

            to_plane(u, low)

        @pl.when(high < zs)
        def _():
            dn_copy(u, high).wait_recv()

            @pl.when(z > 0)
            def _():
                dn_copy(u, high).start()

            to_plane(u, high)

    def partner_copy(u, d):
        slot = slot_of(core, lax.rem(row - d + rows, rows))
        return send(rowbuf.at[u, slot], rowbuf.at[u, slot], dd_send.at[u, d], dd_recv.at[u, d], (row, col + 1 - 2 * core))

    def spread_half(u):
        pltpu.make_async_copy(zbuf.at[u, row], rowbuf.at[u, slot_of(core, row)], own_sem.at[u]).wait()
        partner_copy(u, 0).start()
        for d in range(1, rows):
            plane_copy(u, row, slot_of(core, row), d).wait_recv()
            partner_copy(u, d).start()

    def spread_rest(u):
        for d in range(rows):
            partner_copy(u, d).wait_recv()

    def spread_drain(u):
        for d in range(rows):
            partner_copy(u, d).wait_send()
        for d in range(1, rows):
            plane_copy(u, row, slot_of(core, row), d).wait_send()

        for s in range(zs):
            @pl.when((z + 1 < zs) & (z >= s))
            def _():
                up_copy(u, s).wait_send()

            @pl.when((z > 0) & (z <= s))
            def _():
                dn_copy(u, s).wait_send()

    def ar_refs(u, m):
        deep = width * m // plane
        return deep, pl.ds(0, deep)

    def ar_one(u, m, d):
        deep, span = ar_refs(u, m)
        t = lax.rem(q + d, plane)
        return send(
            a_loc.at[u, t, span], a_in.at[u, d - 1, span], a_s1.at[u, d - 1], a_r1.at[u, d - 1], (t // 2, 2 * z + t % 2)
        )

    def ar_two(u, m, d):
        deep, span = ar_refs(u, m)
        t = lax.rem(z + d, zs)
        return send(
            a_z.at[u, z, span], a_z.at[u, z, span], a_s2.at[u, d - 1], a_r2.at[u, d - 1], (row, 2 * t + core)
        )

    def ar_three(u, m, d):
        deep, span = ar_refs(u, m)
        t = lax.rem(q + d, plane)
        return send(
            a_full.at[u, q, span], a_full.at[u, q, span], a_s3.at[u, d - 1], a_r3.at[u, d - 1],
            (t // 2, 2 * z + t % 2),
        )

    def ar_start(u, m, value):
        deep, span = ar_refs(u, m)
        for t in range(plane):
            a_loc[u, t, span] = value[t * deep : (t + 1) * deep]
        for d in range(1, plane):
            ar_one(u, m, d).start()

    def ar_mid(u, m):
        deep, span = ar_refs(u, m)
        total = a_loc[u, q, span]
        for d in range(1, plane):
            ar_one(u, m, d).wait_recv()
            total = total + a_in[u, d - 1, span]
        a_z[u, z, span] = total
        for d in range(1, zs):
            ar_two(u, m, d).start()

    def ar_late(u, m):
        deep, span = ar_refs(u, m)
        for d in range(1, zs):
            ar_two(u, m, d).wait_recv()
        total = a_z[u, 0, span]
        for s in range(1, zs):
            total = total + a_z[u, s, span]
        a_full[u, q, span] = total
        for d in range(1, plane):
            ar_three(u, m, d).start()

    def ar_finish(u, m):
        deep, span = ar_refs(u, m)
        for d in range(1, plane):
            ar_three(u, m, d).wait_recv()
        value = jnp.concatenate([a_full[u, t, span] for t in range(plane)], axis=0)
        for d in range(1, plane):
            ar_one(u, m, d).wait_send()
            ar_three(u, m, d).wait_send()
        for d in range(1, zs):
            ar_two(u, m, d).wait_send()
        return value

    def all_sum(u, m, value):
        ar_start(u, m, value)
        ar_mid(u, m)
        ar_late(u, m)
        return ar_finish(u, m)

    deep = stage.shape[1]
    chunks = cov_ref.shape[0] // deep

    def fetch(i):
        return pltpu.make_async_copy(cov_ref.at[pl.ds(i * deep, deep), :], stage.at[i % 2], stage_sem.at[i % 2])

    def load_covariance():
        def chunk(i, carry):
            @pl.when(i + 1 < chunks)
            def _():
                fetch(i + 1).start()

            fetch(i).wait()

            def split(s, inner):
                for n in range(rows):
                    high, low = halves(stage[i % 2, pl.ds(s * 16, 16), n * wide : (n + 1) * wide])
                    ahi[n, pl.ds(i * deep + s * 16, 16), :] = high
                    alo[n, pl.ds(i * deep + s * 16, 16), :] = low
                return inner

            lax.fori_loop(0, deep // 16, split, 0, unroll=2)
            return carry

        lax.fori_loop(0, chunks, chunk, 0)

    def multiply(u, first, j):
        high, low = halves(rowbuf[u, j])
        both = jnp.concatenate([high, low], axis=0)

        def column(n, carry):
            span = pl.ds(pl.multiple_of(j * wide, wide), wide)
            go = functools.partial(lax.dot_general, dimension_numbers=NN, preferred_element_type=F32)
            one = go(both, ahi[n, span, :])
            two = go(high, alo[n, span, :])
            value = one[:width] + one[width:] + two
            part[u, n] = jnp.where(first, value, value + part[u, n])
            return carry

        lax.fori_loop(0, rows, column, 0)

    def product(u):
        lax.fori_loop(0, rows, lambda i, c: (multiply(u, i == 0, core * rows + i), c)[1], 0)
        spread_rest(u)
        lax.fori_loop(0, rows, lambda i, c: (multiply(u, False, (1 - core) * rows + i), c)[1], 0)

    def spread_wait(u):
        for s in range(1, zs):
            spread_step(u, s)
        spread_half(u)

    fetch(0).start()
    rs_start(0, x_ref)
    part[0] = jnp.zeros(part.shape[1:], F32)
    part[1] = jnp.zeros(part.shape[1:], F32)
    load_covariance()
    start = rs_finish(0, x_ref)
    spread_start(0, start)
    gram = all_sum(0, 1, dot(start, start, NT))
    upper0, inv0 = factor(gram, work)
    small_ref[0] = upper0
    small_ref[1] = inv0
    q0 = dot(inv0, start, NN)
    spread_wait(0)
    product(0)
    rs_start(1, part.at[0])
    image = rs_finish(1, part.at[0])
    image0 = dot(inv0, image, NN)
    h1 = all_sum(1, 1, dot(q0, image0, NT))
    once = image0 - dot(h1, q0, TN)
    spread_start(1, once)
    both = all_sum(2, 2, jnp.concatenate([dot(q0, once, NT), dot(once, once, NT)], axis=0))
    h2, raw = both[:width], both[width:]
    gram = raw - dot(h2, h2, TN)
    upper1, inv1 = factor(gram, work)
    small_ref[2] = h1
    small_ref[3] = h2
    small_ref[4] = upper1
    small_ref[5] = inv1
    twice = once - dot(h2, q0, TN)
    q1 = dot(inv1, twice, NN)
    spread_wait(1)
    product(1)
    rs_start(2, part.at[1])
    image = rs_finish(2, part.at[1])
    image1 = dot(inv1, image - dot(h2, image0, TN), NN)
    spread_start(2, image1)
    stacked = jnp.concatenate([q0, q1], axis=0)
    g1 = all_sum(3, 2, dot(stacked, image1, NT))
    once = image1 - dot(g1, stacked, TN)
    both = all_sum(4, 3, jnp.concatenate([dot(stacked, once, NT), dot(once, once, NT)], axis=0))
    g2, raw = both[: 2 * width], both[2 * width :]
    gram = raw - dot(g2, g2, TN)
    spread_wait(2)
    upper2, inv2 = factor(gram, work)
    small_ref[6] = g1[:width]
    small_ref[7] = g1[width:]
    small_ref[8] = g2[:width]
    small_ref[9] = g2[width:]
    small_ref[10] = upper2
    small_ref[11] = inv2
    spread_rest(2)
    for u in range(3):
        pltpu.make_async_copy(rowbuf.at[u], wide_ref.at[u], out_sem.at[u]).start()
    for u in range(3):
        spread_drain(u)
    for u in range(3):
        pltpu.make_async_copy(rowbuf.at[u], wide_ref.at[u], out_sem.at[u]).wait()


def main(rows, cols, x, covariance):
    row_count, col_count = covariance.shape
    width, wide = x.shape[1:]
    zs, plane = cols // 2, 2 * rows
    deep = min(256, row_count)
    dma = pltpu.SemaphoreType.DMA
    uses = 3
    sums, most = 5, 3 * width // plane
    return pl.pallas_call(
        functools.partial(main_kernel, rows, cols),
        out_shape=(
            jax.ShapeDtypeStruct((3, cols, width, wide), F32),
            jax.ShapeDtypeStruct((12, width, width), F32),
        ),
        in_specs=[pl.BlockSpec(memory_space=pltpu.VMEM), pl.BlockSpec(memory_space=pl.ANY)],
        out_specs=(pl.BlockSpec(memory_space=pl.ANY), pl.BlockSpec(memory_space=pltpu.VMEM)),
        scratch_shapes=[
            pltpu.VMEM((rows, row_count, wide), BF16),
            pltpu.VMEM((rows, row_count, wide), BF16),
            pltpu.VMEM((2, deep, col_count), F32),
            dma((2,)),
            pltpu.VMEM((2, rows, width, wide), F32),
            pltpu.VMEM((uses, rows - 1, width, wide), F32),
            dma((uses, rows - 1)), dma((uses, rows - 1)),
            pltpu.VMEM((uses, zs, width, wide), F32),
            dma((uses, zs)), dma((uses, zs)), dma((uses, zs)), dma((uses, zs)),
            pltpu.VMEM((uses, cols, width, wide), F32),
            dma((uses, rows)), dma((uses, rows)), dma((uses, rows)), dma((uses, rows)), dma((uses,)), dma((uses,)),
            pltpu.VMEM((sums, plane, most, width), F32),
            pltpu.VMEM((sums, plane - 1, most, width), F32),
            pltpu.VMEM((sums, zs, most, width), F32),
            pltpu.VMEM((sums, plane, most, width), F32),
            dma((sums, plane - 1)), dma((sums, plane - 1)),
            dma((sums, zs - 1)), dma((sums, zs - 1)),
            dma((sums, plane - 1)), dma((sums, plane - 1)),
            pltpu.VMEM((width, 2 * width), F32),
        ],
        compiler_params=pltpu.CompilerParams(collective_id=0, has_side_effects=True, vmem_limit_bytes=LIMIT),
        name="lanczos",
    )(x, covariance)


def finish_kernel(root, wide_ref, small_ref, basis_ref, projection_ref, first_ref):
    width = small_ref.shape[1]
    get = lambda i: small_ref[i]
    upper0, inv0, h1, h2, upper1, inv1, g1a, g1b, g2a, g2b, upper2, inv2 = [get(i) for i in range(12)]
    q0 = dot3(inv0, wide_ref[0, 0], NN)
    q1 = dot3(inv1, wide_ref[1, 0] - dot3(h2, q0, TN), NN)
    stacked = jnp.concatenate([q0, q1], axis=0)
    once = wide_ref[2, 0] - dot3(jnp.concatenate([g1a, g1b], axis=0), stacked, TN)
    twice = once - dot3(jnp.concatenate([g2a, g2b], axis=0), stacked, TN)
    q2 = dot3(inv2, twice, NN)
    for i, value in enumerate((q0, q1, q2)):
        basis_ref[:, i * width : (i + 1) * width] = value.T * root

    @pl.when(pl.program_id(0) == 0)
    def _():
        zero = jnp.zeros((width, width), F32)
        spot = lambda i: pl.ds(i * width, width)
        for r, c, value in (
            (0, 0, h1 + h2), (1, 0, upper1), (2, 0, zero),
            (0, 1, g1a + g2a), (1, 1, g1b + g2b), (2, 1, upper2),
        ):
            projection_ref[spot(r), spot(c)] = value
        for r, c, value in ((0, 0, h1), (1, 0, zero), (2, 0, zero), (0, 1, g1a), (1, 1, g1b), (2, 1, zero)):
            first_ref[spot(r), spot(c)] = value


def finish(order, wide_blocks, small):
    _, cols, width, wide = wide_blocks.shape
    whole = lambda i: (0, 0)
    return pl.pallas_call(
        functools.partial(finish_kernel, float(order) ** 0.5),
        grid=(cols,),
        out_shape=(
            jax.ShapeDtypeStruct((cols * wide, 3 * width), F32),
            jax.ShapeDtypeStruct((3 * width, 2 * width), F32),
            jax.ShapeDtypeStruct((3 * width, 2 * width), F32),
        ),
        in_specs=[
            pl.BlockSpec((3, 1, width, wide), lambda i: (0, i, 0, 0)),
            pl.BlockSpec(small.shape, lambda i: (0, 0, 0)),
        ],
        out_specs=(
            pl.BlockSpec((wide, 3 * width), lambda i: (i, 0)),
            pl.BlockSpec((3 * width, 2 * width), whole),
            pl.BlockSpec((3 * width, 2 * width), whole),
        ),
        compiler_params=pltpu.CompilerParams(vmem_limit_bytes=32 * 1024 * 1024),
        name="finish",
    )(wide_blocks, small)


def solve(rows, cols, covariance, seed_index):
    x = gather(rows, covariance, seed_index)
    wide_blocks, small = main(rows, cols, x, covariance)
    return finish(rows * covariance.shape[0], wide_blocks, small)


def solution(mesh):
    rows, cols = mesh.shape["row"], mesh.shape["col"]
    return jax.shard_map(
        lambda covariance, seed_index: solve(rows, cols, covariance, seed_index),
        mesh=mesh,
        in_specs=(P("row", "col"), P()),
        out_specs=(P("row", None), P(), P()),
        check_vma=False,
    )
```

time: 481 us -> 324 us (0.67)
  the two profiles are of different devices: /device:TPU:0 before, /device:TPU:7 now
where the time goes in v1:
time: 324 us; the launch traced here: 323 us
  Pallas kernels  306 us (94%)
  local copies, waits for them, and re-layouts  15.5 us (5%)
    pallas_call x1, Pallas kernels, main(): pl.pallas_call(functools.partial(main_kernel, rows, cols), out_shape=(jax...  290 us
    unnamed x8, local copies, waits for them, and re-layouts  15.4 us
    pallas_call x1, Pallas kernels, finish(): pl.pallas_call(functools.partial(finish_kernel, float(order) ** 0.5), gri...  13.4 us

profile of v1, /device:TPU:7, one launch (start us, length us, event | category | flops | bytes accessed | tf_op | source)
XLA Modules:
  0.0 323.1 jit_solution(14440399083109576230)
XLA Ops:
  0.6 0.7 fusion
  1.3 0.7 subtract_clamp_fusion.index_ref
  2.0 0.1 copy.5.inside_ref
  2.1 0.0 copy-start
  2.1 10.5 %copy-done = f32[4096,2048]{1,0:T(8,128)S(1)} copy-done((f32[4096,2048]{1,0:T(8,128)S(1)}, f32[4096,2048]{1,0:T(8,128)}, u32[]{:S(2)}) %copy-start) | copy-done | bytes 33554456
  12.6 2.3 gather.1.x_ref
  14.9 0.0 copy-start.2
  14.9 1.0 copy-done.2
  15.9 289.9 %lanczos.1 = (f32[3,8,128,512]{3,2,1,0:T(8,128)}, f32[12,128,128]{2,1,0:T(8,128)}) custom-call(f32[4,128,512]{2,1,0:T(8,128)} %copy-done.2, f32[4096,2048]{1,0:T(8,128)} %cov_ref.3), custom_call_target="tpu_custom_call" | custom-call | tf_op jit(solution)/shard_map/lanczos/pallas_call | solution.py:426
  305.8 0.0 copy-start.1
  305.8 2.8 copy-done.1
  308.6 0.0 copy-start.3
  308.6 1.1 copy-done.3
  309.7 13.4 %finish.1 = (f32[4096,384]{1,0:T(8,128)}, f32[384,256]{1,0:T(8,128)}, f32[384,256]{1,0:T(8,128)}) custom-call(f32[3,8,128,512]{3,2,1,0:T(8,128)S(1)} %copy-done.1, f32[12,128,128]{2,1,0:T(8,128)S(1)} %copy-done.3), custom_call_target="tpu_custom_call" | custom-call | tf_op jit(solution)/shard_map/finish/pallas_call | solution.py:489
Async XLA Ops:
  2.1 10.5 %copy-start = (f32[4096,2048]{1,0:T(8,128)S(1)}, f32[4096,2048]{1,0:T(8,128)}, u32[]{:S(2)}) copy-start(f32[4096,2048]{1,0:T(8,128)} %cov_ref.3) | copy-start | bytes 100663296
  14.9 1.0 copy-start.2
  305.8 2.8 copy-start.1
  308.6 1.1 copy-start.3

commit v2 on v1

--- a/solution.py
+++ b/solution.py
@@ -9,7 +9,7 @@
 
 MESH = pl.DeviceIdType.MESH
 F32, BF16 = jnp.float32, jnp.bfloat16
-ITERS = 2
+PARTS = 2
 LIMIT = 66 * 1024 * 1024 - 2 * 1024 * 1024
 
 NN = (((1,), (0,)), ((), ()))
@@ -63,33 +63,48 @@
         ],
         out_specs=pl.BlockSpec(memory_space=pltpu.VMEM),
         scratch_shapes=[pltpu.VMEM((width, cols), F32), pltpu.SemaphoreType.DMA],
-        compiler_params=pltpu.CompilerParams(vmem_limit_bytes=8 * 1024 * 1024),
+        compiler_params=pltpu.CompilerParams(vmem_limit_bytes=LIMIT),
         name="gather",
     )(jnp.clip(offsets, 0, row_count - 1), inside.astype(jnp.int32)[:, None], covariance)
 
 
 def factor(gram, work):
     width = gram.shape[0]
+    deep = 8
     down = lax.broadcasted_iota(jnp.int32, (width, width), 0)
     across = lax.broadcasted_iota(jnp.int32, (width, width), 1)
+    few = lax.broadcasted_iota(jnp.int32, (deep, width), 1)
+    tall = lax.broadcasted_iota(jnp.int32, (width, 1), 0)
+    short = lax.broadcasted_iota(jnp.int32, (deep, 1), 0)
     work[:, :width] = gram
     work[:, width:] = jnp.where(down == across, 1.0, 0.0)
-    lane = lax.broadcasted_iota(jnp.int32, (1, width), 1)
-    tall = lax.broadcasted_iota(jnp.int32, (width, 1), 0)
-
-    def step(j, carry):
-        row = work[pl.ds(j, 1), :]
-        pivot = jnp.sum(jnp.where(lane == j, row[:, :width], 0.0), axis=1, keepdims=True)
+
+    def panel(p, carry):
+        base = pl.multiple_of(p * deep, deep)
+        block = work[pl.ds(base, deep), :]
         now = work[...]
-        column = jnp.sum(jnp.where(across == j, now[:, :width], 0.0), axis=1, keepdims=True)
-        scale = lax.rsqrt(pivot)
-        scale = scale * (1.5 - 0.5 * pivot * scale * scale)
-        unit = row * scale
-        ratio = jnp.where(tall > j, column * scale, 0.0)
-        work[...] = jnp.where(tall == j, unit, now - ratio * unit)
+        left, top = now[:, :width], block[:, :width]
+        small = [jnp.sum(jnp.where(few == base + t, top, 0.0), axis=1, keepdims=True) for t in range(deep)]
+        large = [jnp.sum(jnp.where(across == base + t, left, 0.0), axis=1, keepdims=True) for t in range(deep)]
+        for t in range(deep):
+            pivot = small[t][t : t + 1]
+            scale = lax.rsqrt(pivot)
+            scale = scale * (1.5 - 0.5 * pivot * scale * scale)
+            unit = block[t : t + 1] * scale
+            column = small[t] * scale
+            large[t] = large[t] * scale
+            for e in range(t + 1, deep):
+                factor_e = column[e : e + 1]
+                small[e] = small[e] - column * factor_e
+                large[e] = large[e] - large[t] * factor_e
+            block = jnp.where(short == t, unit, block - jnp.where(short > t, column, 0.0) * unit)
+        for t in range(deep):
+            now = now - jnp.where(tall >= base + deep, large[t], 0.0) * block[t : t + 1]
+        work[...] = now
+        work[pl.ds(base, deep), :] = block
         return carry
 
-    lax.fori_loop(0, width, step, 0)
+    lax.fori_loop(0, width // deep, panel, 0)
     upper = jnp.where(down <= across, work[:, :width], 0.0)
     return upper, work[:, width:]
 
@@ -99,7 +114,7 @@
     wide_ref, small_ref,
     ahi, alo, stage, stage_sem, part, rsbuf, rs_send, rs_recv,
     zbuf, up_send, up_recv, dn_send, dn_recv, rowbuf, pl_send, pl_recv, dd_send, dd_recv, own_sem, out_sem,
-    a_loc, a_in, a_z, a_full, a_s1, a_r1, a_s2, a_r2, a_s3, a_r3, work,
+    a_loc, a_in, a_z, a_full, a_s1, a_r1, a_s2, a_r2, a_s3, a_r3, work, wsplit,
 ):
     zs = cols // 2
     width, wide = x_ref.shape[1], x_ref.shape[2]
@@ -110,6 +125,13 @@
     plane = 2 * rows
     q = row * 2 + core
 
+    deep = stage.shape[1]
+    chunks = cov_ref.shape[0] // deep
+
+    def fetch(i):
+        return pltpu.make_async_copy(cov_ref.at[pl.ds(i * deep, deep), :], stage.at[i % 2], stage_sem.at[i % 2])
+
+    fetch(0).start()
     barrier = pltpu.get_barrier_semaphore()
     for d in range(1, plane):
         t = lax.rem(q + d, plane)
@@ -126,16 +148,17 @@
             src_ref=src, dst_ref=dst, send_sem=ssem, recv_sem=rsem, device_id=dev, device_id_type=MESH
         )
 
+    def rs_copy(u, src, d):
+        t = lax.rem(row + d, rows)
+        return send(src.at[t], rsbuf.at[u, d - 1], rs_send.at[u, d - 1], rs_recv.at[u, d - 1], (t, col))
+
     def rs_copies(u, src):
-        out = []
-        for d in range(1, rows):
-            t = lax.rem(row + d, rows)
-            out.append(send(src.at[t], rsbuf.at[u, d - 1], rs_send.at[u, d - 1], rs_recv.at[u, d - 1], (t, col)))
-        return out
+        return [rs_copy(u, src, d) for d in range(1, rows)]
 
     def rs_start(u, src):
         for copy in rs_copies(u, src):
             copy.start()
+
 
     def rs_finish(u, src):
         total = src[row]
@@ -146,92 +169,108 @@
             copy.wait_send()
         return total
 
-    def up_copy(u, s):
-        return send(zbuf.at[u, s], zbuf.at[u, s], up_send.at[u, s], up_recv.at[u, s], (row, col + 2))
-
-    def dn_copy(u, s):
-        return send(zbuf.at[u, s], zbuf.at[u, s], dn_send.at[u, s], dn_recv.at[u, s], (row, col - 2))
-
-    def plane_copy(u, t, slot, d):
-        return send(zbuf.at[u, t], rowbuf.at[u, slot], pl_send.at[u, d], pl_recv.at[u, d], (t, col))
+    parts = up_send.shape[2]
+    thick = width // parts
+
+    def part_of(h):
+        return pl.ds(h * thick, thick)
+
+    def up_copy(u, s, h):
+        ref = zbuf.at[u, s, part_of(h)]
+        return send(ref, ref, up_send.at[u, s, h], up_recv.at[u, s, h], (row, col + 2))
+
+    def dn_copy(u, s, h):
+        ref = zbuf.at[u, s, part_of(h)]
+        return send(ref, ref, dn_send.at[u, s, h], dn_recv.at[u, s, h], (row, col - 2))
 
     def slot_of(k, r):
         return k * rows + r
 
-    def to_plane(u, s):
+    def plane_copy(u, t, h, d):
+        dst = rowbuf.at[u, slot_of(core, row), part_of(h)]
+        return send(zbuf.at[u, t, part_of(h)], dst, pl_send.at[u, d, h], pl_recv.at[u, d, h], (t, col))
+
+    def own_copy(u):
+        return pltpu.make_async_copy(zbuf.at[u, row], rowbuf.at[u, slot_of(core, row)], own_sem.at[u])
+
+    def to_plane(u, s, h):
         @pl.when(s != row)
         def _():
-            plane_copy(u, s, slot_of(core, row), lax.rem(s - row + rows, rows)).start()
-
-        @pl.when(s == row)
-        def _():
-            pltpu.make_async_copy(zbuf.at[u, s], rowbuf.at[u, slot_of(core, row)], own_sem.at[u]).start()
+            plane_copy(u, s, h, lax.rem(s - row + rows, rows)).start()
+
+        if h == parts - 1:
+            @pl.when(s == row)
+            def _():
+                own_copy(u).start()
 
     def spread_start(u, piece):
         zbuf[u, z] = piece
-
-        @pl.when(z + 1 < zs)
-        def _():
-            up_copy(u, z).start()
-
-        @pl.when(z > 0)
-        def _():
-            dn_copy(u, z).start()
-
-        to_plane(u, z)
+        for h in range(parts):
+            @pl.when(z + 1 < zs)
+            def _():
+                up_copy(u, z, h).start()
+
+            @pl.when(z > 0)
+            def _():
+                dn_copy(u, z, h).start()
+
+            to_plane(u, z, h)
 
     def spread_step(u, s):
         low, high = z - s, z + s
-
-        @pl.when(low >= 0)
-        def _():
-            up_copy(u, low).wait_recv()
-
-            @pl.when(z + 1 < zs)
+        for h in range(parts):
+            @pl.when(low >= 0)
             def _():
-                up_copy(u, low).start()
-
-            to_plane(u, low)
-
-        @pl.when(high < zs)
-        def _():
-            dn_copy(u, high).wait_recv()
-
-            @pl.when(z > 0)
+                up_copy(u, low, h).wait_recv()
+
+                @pl.when(z + 1 < zs)
+                def _():
+                    up_copy(u, low, h).start()
+
+                to_plane(u, low, h)
+
+            @pl.when(high < zs)
             def _():
-                dn_copy(u, high).start()
-
-            to_plane(u, high)
-
-    def partner_copy(u, d):
-        slot = slot_of(core, lax.rem(row - d + rows, rows))
-        return send(rowbuf.at[u, slot], rowbuf.at[u, slot], dd_send.at[u, d], dd_recv.at[u, d], (row, col + 1 - 2 * core))
+                dn_copy(u, high, h).wait_recv()
+
+                @pl.when(z > 0)
+                def _():
+                    dn_copy(u, high, h).start()
+
+                to_plane(u, high, h)
+
+    def partner_copy(u, d, h):
+        ref = rowbuf.at[u, slot_of(core, lax.rem(row - d + rows, rows)), part_of(h)]
+        return send(ref, ref, dd_send.at[u, d, h], dd_recv.at[u, d, h], (row, col + 1 - 2 * core))
 
     def spread_half(u):
-        pltpu.make_async_copy(zbuf.at[u, row], rowbuf.at[u, slot_of(core, row)], own_sem.at[u]).wait()
-        partner_copy(u, 0).start()
-        for d in range(1, rows):
-            plane_copy(u, row, slot_of(core, row), d).wait_recv()
-            partner_copy(u, d).start()
+        own_copy(u).wait()
+        for h in range(parts):
+            partner_copy(u, 0, h).start()
+        for h in range(parts):
+            for d in range(1, rows):
+                plane_copy(u, row, h, d).wait_recv()
+                partner_copy(u, d, h).start()
 
     def spread_rest(u):
-        for d in range(rows):
-            partner_copy(u, d).wait_recv()
+        for h in range(parts):
+            for d in range(rows):
+                partner_copy(u, d, h).wait_recv()
 
     def spread_drain(u):
-        for d in range(rows):
-            partner_copy(u, d).wait_send()
-        for d in range(1, rows):
-            plane_copy(u, row, slot_of(core, row), d).wait_send()
-
-        for s in range(zs):
-            @pl.when((z + 1 < zs) & (z >= s))
-            def _():
-                up_copy(u, s).wait_send()
-
-            @pl.when((z > 0) & (z <= s))
-            def _():
-                dn_copy(u, s).wait_send()
+        for h in range(parts):
+            for d in range(rows):
+                partner_copy(u, d, h).wait_send()
+            for d in range(1, rows):
+                plane_copy(u, row, h, d).wait_send()
+            for s in range(zs):
+                @pl.when((z + 1 < zs) & (z >= s))
+                def _():
+                    up_copy(u, s, h).wait_send()
+
+                @pl.when((z > 0) & (z <= s))
+                def _():
+                    dn_copy(u, s, h).wait_send()
 
     def ar_refs(u, m):
         deep = width * m // plane
@@ -305,13 +344,7 @@
         ar_late(u, m)
         return ar_finish(u, m)
 
-    deep = stage.shape[1]
-    chunks = cov_ref.shape[0] // deep
-
-    def fetch(i):
-        return pltpu.make_async_copy(cov_ref.at[pl.ds(i * deep, deep), :], stage.at[i % 2], stage_sem.at[i % 2])
-
-    def load_covariance():
+    def load_covariance(begin, end):
         def chunk(i, carry):
             @pl.when(i + 1 < chunks)
             def _():
@@ -326,93 +359,174 @@
                     alo[n, pl.ds(i * deep + s * 16, 16), :] = low
                 return inner
 
-            lax.fori_loop(0, deep // 16, split, 0, unroll=2)
+            lax.fori_loop(0, deep // 16, split, 0, unroll=4)
             return carry
 
-        lax.fori_loop(0, chunks, chunk, 0)
-
-    def multiply(u, first, j):
+        lax.fori_loop(begin, end, chunk, 0)
+
+    def term(n, span, high, both):
+        go = functools.partial(lax.dot_general, dimension_numbers=NN, preferred_element_type=F32)
+        one = go(both, ahi[n, span, :])
+        two = go(high, alo[n, span, :])
+        return one[:width] + one[width:] + two
+
+    def split_rows(u, j):
         high, low = halves(rowbuf[u, j])
-        both = jnp.concatenate([high, low], axis=0)
-
-        def column(n, carry):
-            span = pl.ds(pl.multiple_of(j * wide, wide), wide)
-            go = functools.partial(lax.dot_general, dimension_numbers=NN, preferred_element_type=F32)
-            one = go(both, ahi[n, span, :])
-            two = go(high, alo[n, span, :])
-            value = one[:width] + one[width:] + two
-            part[u, n] = jnp.where(first, value, value + part[u, n])
+        wsplit[j, :width] = high
+        wsplit[j, width:] = low
+
+    def span_of(j):
+        return pl.ds(pl.multiple_of(j * wide, wide), wide)
+
+    def product_near(u):
+        def piece(i, carry):
+            j = core * rows + i
+            split_rows(u, j)
+            for n in range(rows):
+                value = term(n, span_of(j), wsplit[j, :width], wsplit[j])
+                part[u, n] = jnp.where(i == 0, value, value + part[u, n])
             return carry
 
-        lax.fori_loop(0, rows, column, 0)
-
-    def product(u):
-        lax.fori_loop(0, rows, lambda i, c: (multiply(u, i == 0, core * rows + i), c)[1], 0)
-        spread_rest(u)
-        lax.fori_loop(0, rows, lambda i, c: (multiply(u, False, (1 - core) * rows + i), c)[1], 0)
-
-    def spread_wait(u):
-        for s in range(1, zs):
-            spread_step(u, s)
-        spread_half(u)
-
-    fetch(0).start()
-    rs_start(0, x_ref)
-    part[0] = jnp.zeros(part.shape[1:], F32)
-    part[1] = jnp.zeros(part.shape[1:], F32)
-    load_covariance()
-    start = rs_finish(0, x_ref)
-    spread_start(0, start)
-    gram = all_sum(0, 1, dot(start, start, NT))
-    upper0, inv0 = factor(gram, work)
-    small_ref[0] = upper0
-    small_ref[1] = inv0
-    q0 = dot(inv0, start, NN)
-    spread_wait(0)
-    product(0)
-    rs_start(1, part.at[0])
-    image = rs_finish(1, part.at[0])
-    image0 = dot(inv0, image, NN)
-    h1 = all_sum(1, 1, dot(q0, image0, NT))
-    once = image0 - dot(h1, q0, TN)
-    spread_start(1, once)
-    both = all_sum(2, 2, jnp.concatenate([dot(q0, once, NT), dot(once, once, NT)], axis=0))
-    h2, raw = both[:width], both[width:]
-    gram = raw - dot(h2, h2, TN)
-    upper1, inv1 = factor(gram, work)
-    small_ref[2] = h1
-    small_ref[3] = h2
-    small_ref[4] = upper1
-    small_ref[5] = inv1
-    twice = once - dot(h2, q0, TN)
-    q1 = dot(inv1, twice, NN)
-    spread_wait(1)
-    product(1)
-    rs_start(2, part.at[1])
-    image = rs_finish(2, part.at[1])
-    image1 = dot(inv1, image - dot(h2, image0, TN), NN)
-    spread_start(2, image1)
-    stacked = jnp.concatenate([q0, q1], axis=0)
-    g1 = all_sum(3, 2, dot(stacked, image1, NT))
-    once = image1 - dot(g1, stacked, TN)
-    both = all_sum(4, 3, jnp.concatenate([dot(stacked, once, NT), dot(once, once, NT)], axis=0))
-    g2, raw = both[: 2 * width], both[2 * width :]
-    gram = raw - dot(g2, g2, TN)
-    spread_wait(2)
-    upper2, inv2 = factor(gram, work)
-    small_ref[6] = g1[:width]
-    small_ref[7] = g1[width:]
-    small_ref[8] = g2[:width]
-    small_ref[9] = g2[width:]
-    small_ref[10] = upper2
-    small_ref[11] = inv2
-    spread_rest(2)
-    for u in range(3):
-        pltpu.make_async_copy(rowbuf.at[u], wide_ref.at[u], out_sem.at[u]).start()
-    for u in range(3):
-        spread_drain(u)
-    for u in range(3):
-        pltpu.make_async_copy(rowbuf.at[u], wide_ref.at[u], out_sem.at[u]).wait()
+        lax.fori_loop(0, rows, piece, 0)
+
+    def product_far(u, rs):
+        lax.fori_loop(0, rows, lambda i, c: (split_rows(u, (1 - core) * rows + i), c)[1], 0)
+
+        def target(d, carry):
+            n = lax.rem(row + d, rows)
+            value = part[u, n]
+            for i in range(rows):
+                j = (1 - core) * rows + i
+                value = value + term(n, span_of(j), wsplit[j, :width], wsplit[j])
+            part[u, n] = value
+
+            @pl.when(d < rows)
+            def _():
+                rs_copy(rs, part.at[u], d).start()
+
+            return carry
+
+        lax.fori_loop(1, rows + 1, target, 0)
+
+    def scope(name):
+        return jax.named_scope(name)
+
+    def rows_to_basis(u, inverse, other):
+        def piece(j, carry):
+            value = rowbuf[u, j]
+            if other is not None:
+                value = value - dot3(other, rowbuf[0, j], TN)
+            rowbuf[u, j] = dot3(inverse, value, NN)
+            return carry
+
+        lax.fori_loop(0, cols, piece, 0)
+        wide_copy(u).start()
+
+    def wide_copy(u):
+        return pltpu.make_async_copy(rowbuf.at[u], wide_ref.at[u], out_sem.at[u])
+
+    def spread_and_multiply(u, block, a, m, small):
+        with scope(f"spread_start#{u}"):
+            spread_start(u, block)
+            ar_start(a, m, small())
+        if u == 0:
+            with scope("load_rest#0"):
+                load_covariance(chunks // 2, chunks)
+        with scope(f"spread_step#{u}"):
+            for s in range(1, zs):
+                spread_step(u, s)
+        with scope(f"spread_half#{u}"):
+            ar_mid(a, m)
+            spread_half(u)
+        with scope(f"near#{u}"):
+            product_near(u)
+        with scope(f"spread_rest#{u}"):
+            ar_late(a, m)
+            spread_rest(u)
+        with scope(f"far#{u}"):
+            product_far(u, u + 1)
+
+    with scope("start#0"):
+        rs_start(0, x_ref)
+        load_covariance(0, chunks // 2)
+    with scope("rs#0"):
+        start = rs_finish(0, x_ref)
+    spread_and_multiply(0, start, 0, 1, lambda: dot(start, start, NT))
+    with scope("factor#0"):
+        gram = ar_finish(0, 1)
+        upper0, inv0 = factor(gram, work)
+        small_ref[0] = upper0
+        small_ref[1] = inv0
+        q0 = dot(inv0, start, NN)
+    with scope("rs#1"):
+        image = rs_finish(1, part.at[0])
+    with scope("sum#1"):
+        image0 = dot(inv0, image, NN)
+        ar_start(1, 1, dot(q0, image0, NT))
+        ar_mid(1, 1)
+        ar_late(1, 1)
+        h1 = ar_finish(1, 1)
+        once = image0 - dot(h1, q0, TN)
+    spread_and_multiply(
+        1, once, 2, 2, lambda: jnp.concatenate([dot(q0, once, NT), dot(once, once, NT)], axis=0)
+    )
+    with scope("factor#1"):
+        both = ar_finish(2, 2)
+        h2, raw = both[:width], both[width:]
+        gram = raw - dot(h2, h2, TN)
+        upper1, inv1 = factor(gram, work)
+        small_ref[2] = h1
+        small_ref[3] = h2
+        small_ref[4] = upper1
+        small_ref[5] = inv1
+        twice = once - dot(h2, q0, TN)
+        q1 = dot(inv1, twice, NN)
+        shift = dot(h2, image0, TN)
+        stacked = jnp.concatenate([q0, q1], axis=0)
+    with scope("rs#2"):
+        image = rs_finish(2, part.at[1])
+    with scope("sum#3"):
+        image1 = dot(inv1, image - shift, NN)
+        ar_start(3, 2, dot(stacked, image1, NT))
+        spread_drain(0)
+        rows_to_basis(0, inv0, None)
+        ar_mid(3, 2)
+        ar_late(3, 2)
+        g1 = ar_finish(3, 2)
+        once = image1 - dot(g1, stacked, TN)
+    with scope("last_start#0"):
+        ar_start(4, 3, jnp.concatenate([dot(stacked, once, NT), dot(once, once, NT)], axis=0))
+        spread_start(2, once)
+    with scope("basis#1"):
+        spread_drain(1)
+        wide_copy(0).wait()
+        rows_to_basis(1, inv1, h2)
+    with scope("last_steps#0"):
+        spread_step(2, 1)
+        ar_mid(4, 3)
+        for s in range(2, zs):
+            spread_step(2, s)
+        ar_late(4, 3)
+    with scope("last_half#0"):
+        spread_half(2)
+    with scope("last_sum#0"):
+        both = ar_finish(4, 3)
+    with scope("factor#2"):
+        g2, raw = both[: 2 * width], both[2 * width :]
+        gram = raw - dot(g2, g2, TN)
+        upper2, inv2 = factor(gram, work)
+        small_ref[6] = g1[:width]
+        small_ref[7] = g1[width:]
+        small_ref[8] = g2[:width]
+        small_ref[9] = g2[width:]
+        small_ref[10] = upper2
+        small_ref[11] = inv2
+    with scope("end#0"):
+        spread_rest(2)
+        wide_copy(2).start()
+        spread_drain(2)
+        wide_copy(1).wait()
+        wide_copy(2).wait()
 
 
 def main(rows, cols, x, covariance):
@@ -440,9 +554,10 @@
             pltpu.VMEM((uses, rows - 1, width, wide), F32),
             dma((uses, rows - 1)), dma((uses, rows - 1)),
             pltpu.VMEM((uses, zs, width, wide), F32),
-            dma((uses, zs)), dma((uses, zs)), dma((uses, zs)), dma((uses, zs)),
+            dma((uses, zs, PARTS)), dma((uses, zs, PARTS)), dma((uses, zs, PARTS)), dma((uses, zs, PARTS)),
             pltpu.VMEM((uses, cols, width, wide), F32),
-            dma((uses, rows)), dma((uses, rows)), dma((uses, rows)), dma((uses, rows)), dma((uses,)), dma((uses,)),
+            dma((uses, rows, PARTS)), dma((uses, rows, PARTS)), dma((uses, rows, PARTS)), dma((uses, rows, PARTS)),
+            dma((uses,)), dma((uses,)),
             pltpu.VMEM((sums, plane, most, width), F32),
             pltpu.VMEM((sums, plane - 1, most, width), F32),
             pltpu.VMEM((sums, zs, most, width), F32),
@@ -451,6 +566,7 @@
             dma((sums, zs - 1)), dma((sums, zs - 1)),
             dma((sums, plane - 1)), dma((sums, plane - 1)),
             pltpu.VMEM((width, 2 * width), F32),
+            pltpu.VMEM((cols, 2 * width, wide), BF16),
         ],
         compiler_params=pltpu.CompilerParams(collective_id=0, has_side_effects=True, vmem_limit_bytes=LIMIT),
         name="lanczos",
@@ -461,12 +577,8 @@
     width = small_ref.shape[1]
     get = lambda i: small_ref[i]
     upper0, inv0, h1, h2, upper1, inv1, g1a, g1b, g2a, g2b, upper2, inv2 = [get(i) for i in range(12)]
-    q0 = dot3(inv0, wide_ref[0, 0], NN)
-    q1 = dot3(inv1, wide_ref[1, 0] - dot3(h2, q0, TN), NN)
-    stacked = jnp.concatenate([q0, q1], axis=0)
-    once = wide_ref[2, 0] - dot3(jnp.concatenate([g1a, g1b], axis=0), stacked, TN)
-    twice = once - dot3(jnp.concatenate([g2a, g2b], axis=0), stacked, TN)
-    q2 = dot3(inv2, twice, NN)
+    q0, q1 = wide_ref[0, 0], wide_ref[1, 0]
+    q2 = dot3(inv2, wide_ref[2, 0] - (dot3(g2a, q0, TN) + dot3(g2b, q1, TN)), NN)
     for i, value in enumerate((q0, q1, q2)):
         basis_ref[:, i * width : (i + 1) * width] = value.T * root
 
@@ -503,7 +615,7 @@
             pl.BlockSpec((3 * width, 2 * width), whole),
             pl.BlockSpec((3 * width, 2 * width), whole),
         ),
-        compiler_params=pltpu.CompilerParams(vmem_limit_bytes=32 * 1024 * 1024),
+        compiler_params=pltpu.CompilerParams(vmem_limit_bytes=LIMIT),
         name="finish",
     )(wide_blocks, small)
 

time: 324 us -> 214 us (0.66)
  Pallas kernels: 306 us -> 210 us
  local copies, waits for them, and re-layouts: 15.5 us -> 0.74 us
    pallas_call x1, Pallas kernels: 290 us -> 193 us  [main(): pl.pallas_call(functools.partial(main_kernel, rows, cols), out_shape=(jax...]
    unnamed x8 -> x0, local copies, waits for them, and re-layouts: 15.4 us -> none
    pallas_call x1, Pallas kernels: 2.31 us -> 5.98 us  [gather(): pl.pallas_call(functools.partial(gather_kernel, rows), out_shape=jax.Shap...]
where the time goes in v2:
time: 214 us; the launch traced here: 213 us
  Pallas kernels  210 us (98%)
    pallas_call x1, Pallas kernels, main(): pl.pallas_call(functools.partial(main_kernel, rows, cols), out_shape=(jax...  193 us
    pallas_call x1, Pallas kernels, finish(): pl.pallas_call(functools.partial(finish_kernel, float(order) ** 0.5), gri...  10.9 us
    pallas_call x1, Pallas kernels, gather(): pl.pallas_call(functools.partial(gather_kernel, rows), out_shape=jax.Shap...  5.98 us

profile of v2, /device:TPU:7, one launch (start us, length us, event | category | flops | bytes accessed | tf_op | source)
XLA Modules:
  0.0 212.8 jit_solution(3777243748310383002)
XLA Ops:
  0.6 0.7 fusion
  1.3 1.2 subtract_clamp_fusion.index_ref
  2.5 0.7 copy.5.inside_ref
  3.2 6.0 %gather.1.x_ref = f32[4,128,512]{2,1,0:T(8,128)} custom-call(s32[128]{0:T(128)} %subtract_clamp_fusion.index_ref, s32[128,1]{1,0:T(8,128)} %copy.5.inside_ref, f32[4096,2048]{1,0:T(8,128)} %cov_ref.3), custom_call_target="tpu_custom_call" | custom-call | tf_op jit(solution)/shard_map/gather/pallas_call | solution.py:56
  9.2 192.7 %lanczos.1 = (f32[3,8,128,512]{3,2,1,0:T(8,128)}, f32[12,128,128]{2,1,0:T(8,128)}) custom-call(f32[4,128,512]{2,1,0:T(8,128)} %gather.1.x_ref, f32[4096,2048]{1,0:T(8,128)} %cov_ref.3), custom_call_target="tpu_custom_call" | custom-call | tf_op jit(solution)/shard_map/lanczos/pallas_call | solution.py:540
  201.9 10.9 %finish.1 = (f32[4096,384]{1,0:T(8,128)}, f32[384,256]{1,0:T(8,128)}, f32[384,256]{1,0:T(8,128)}) custom-call(f32[3,8,128,512]{3,2,1,0:T(8,128)} %get-tuple-element.5.wide_ref, f32[12,128,128]{2,1,0:T(8,128)} %get-tuple-element.6.small_ref), custom_call_target="tpu_custom_call" | custom-call | tf_op jit(solution)/shard_map/finish/pallas_call | solution.py:601

commit v3 on v2

--- a/solution.py
+++ b/solution.py
@@ -9,7 +9,9 @@
 
 MESH = pl.DeviceIdType.MESH
 F32, BF16 = jnp.float32, jnp.bfloat16
-PARTS = 2
+PARTS = 8
+AHEAD = 3
+LAG = 2
 LIMIT = 66 * 1024 * 1024 - 2 * 1024 * 1024
 
 NN = (((1,), (0,)), ((), ()))
@@ -24,6 +26,10 @@
 def halves(value):
     high = value.astype(BF16)
     return high, (value - high.astype(F32)).astype(BF16)
+
+
+def dot1(left, right, dims):
+    return lax.dot_general(left.astype(BF16), right.astype(BF16), dims, preferred_element_type=F32)
 
 
 def dot3(left, right, dims):
@@ -33,51 +39,58 @@
     return go(lh, rh) + (go(lh, rl) + go(ll, rh))
 
 
-def gather_kernel(rows, index_ref, inside_ref, cov_ref, out_ref, buf, sem):
+def gather_kernel(rows, index_ref, cov_ref, out_ref, buf, sem):
     width, cols = buf.shape
     wide = cols // rows
-
-    def fetch(i, carry):
-        pltpu.make_async_copy(cov_ref.at[pl.ds(index_ref[i], 1), :], buf.at[pl.ds(i, 1), :], sem).start()
-        return carry
-
-    lax.fori_loop(0, width, fetch, 0, unroll=8)
+    row_count = cov_ref.shape[0]
+    base = lax.axis_index("row") * row_count
+    tall = lax.broadcasted_iota(jnp.int32, (width, 1), 0)
+
+    def fetch(i, keep):
+        place = index_ref[i]
+        local = lax.rem(place, row_count)
+        pltpu.make_async_copy(cov_ref.at[pl.ds(local, 1), :], buf.at[pl.ds(i, 1), :], sem).start()
+        inside = jnp.where(place - local == base, 1, 0)
+        return jnp.where(tall == i, inside, keep)
+
+    keep = lax.fori_loop(0, width, fetch, jnp.zeros((width, 1), jnp.int32), unroll=8)
     pltpu.make_async_copy(cov_ref.at[pl.ds(0, width), :], buf, sem).wait()
-    keep = inside_ref[...] > 0
     for n in range(rows):
-        out_ref[n] = jnp.where(keep, buf[:, n * wide : (n + 1) * wide], 0.0)
+        out_ref[n] = jnp.where(keep > 0, buf[:, n * wide : (n + 1) * wide], 0.0)
 
 
 def gather(rows, covariance, seed_index):
-    row_count, cols = covariance.shape
+    cols = covariance.shape[1]
     width = seed_index.shape[0]
-    offsets = seed_index - lax.axis_index("row") * row_count
-    inside = (offsets >= 0) & (offsets < row_count)
     return pl.pallas_call(
         functools.partial(gather_kernel, rows),
         out_shape=jax.ShapeDtypeStruct((rows, width, cols // rows), F32),
-        in_specs=[
-            pl.BlockSpec(memory_space=pltpu.SMEM),
-            pl.BlockSpec(memory_space=pltpu.VMEM),
-            pl.BlockSpec(memory_space=pl.ANY),
-        ],
+        in_specs=[pl.BlockSpec(memory_space=pltpu.SMEM), pl.BlockSpec(memory_space=pl.ANY)],
         out_specs=pl.BlockSpec(memory_space=pltpu.VMEM),
         scratch_shapes=[pltpu.VMEM((width, cols), F32), pltpu.SemaphoreType.DMA],
         compiler_params=pltpu.CompilerParams(vmem_limit_bytes=LIMIT),
         name="gather",
-    )(jnp.clip(offsets, 0, row_count - 1), inside.astype(jnp.int32)[:, None], covariance)
-
-
-def factor(gram, work):
+    )(seed_index, covariance)
+
+
+DEEP = 8
+
+
+def factor_begin(gram, work):
     width = gram.shape[0]
-    deep = 8
     down = lax.broadcasted_iota(jnp.int32, (width, width), 0)
+    across = lax.broadcasted_iota(jnp.int32, (width, width), 1)
+    work[:, :width] = gram
+    work[:, width:] = jnp.where(down == across, 1.0, 0.0)
+
+
+def factor_panels(work, begin, end):
+    width = work.shape[0]
+    deep = DEEP
     across = lax.broadcasted_iota(jnp.int32, (width, width), 1)
     few = lax.broadcasted_iota(jnp.int32, (deep, width), 1)
     tall = lax.broadcasted_iota(jnp.int32, (width, 1), 0)
     short = lax.broadcasted_iota(jnp.int32, (deep, 1), 0)
-    work[:, :width] = gram
-    work[:, width:] = jnp.where(down == across, 1.0, 0.0)
 
     def panel(p, carry):
         base = pl.multiple_of(p * deep, deep)
@@ -104,17 +117,28 @@
         work[pl.ds(base, deep), :] = block
         return carry
 
-    lax.fori_loop(0, width // deep, panel, 0)
-    upper = jnp.where(down <= across, work[:, :width], 0.0)
-    return upper, work[:, width:]
+    lax.fori_loop(begin, end, panel, 0)
+
+
+def factor_end(work):
+    width = work.shape[0]
+    down = lax.broadcasted_iota(jnp.int32, (width, width), 0)
+    across = lax.broadcasted_iota(jnp.int32, (width, width), 1)
+    return jnp.where(down <= across, work[:, :width], 0.0), work[:, width:]
+
+
+def factor(gram, work):
+    factor_begin(gram, work)
+    factor_panels(work, 0, work.shape[0] // DEEP)
+    return factor_end(work)
 
 
 def main_kernel(
-    rows, cols, x_ref, cov_ref,
-    wide_ref, small_ref,
-    ahi, alo, stage, stage_sem, part, rsbuf, rs_send, rs_recv,
+    rows, cols, root, x_ref, cov_ref,
+    wide_ref, tall_ref, small_ref,
+    ahi, alo, stage, stage_sem, part, rsbuf, rs_send, rs_recv, st_send, st_recv,
     zbuf, up_send, up_recv, dn_send, dn_recv, rowbuf, pl_send, pl_recv, dd_send, dd_recv, own_sem, out_sem,
-    a_loc, a_in, a_z, a_full, a_s1, a_r1, a_s2, a_r2, a_s3, a_r3, work, wsplit,
+    a_loc, a_in, a_z, a_full, a_s1, a_r1, a_s2, a_r2, a_s3, a_r3, work, wsplit, tall,
 ):
     zs = cols // 2
     width, wide = x_ref.shape[1], x_ref.shape[2]
@@ -203,41 +227,63 @@
             def _():
                 own_copy(u).start()
 
-    def spread_start(u, piece):
+    def spread_put(u, piece):
         zbuf[u, z] = piece
-        for h in range(parts):
+
+    def spread_post(u, h):
+        @pl.when(z + 1 < zs)
+        def _():
+            up_copy(u, z, h).start()
+
+        @pl.when(z > 0)
+        def _():
+            dn_copy(u, z, h).start()
+
+        to_plane(u, z, h)
+
+    ahead = AHEAD
+
+    def spread_step(u, s, h):
+        low, high = z - s, z + s
+
+        @pl.when(low >= 0)
+        def _():
+            up_copy(u, low, h).wait_recv()
+
             @pl.when(z + 1 < zs)
             def _():
-                up_copy(u, z, h).start()
+                up_copy(u, low, h).start()
+
+            to_plane(u, low, h)
+
+        @pl.when(high < zs)
+        def _():
+            dn_copy(u, high, h).wait_recv()
 
             @pl.when(z > 0)
             def _():
-                dn_copy(u, z, h).start()
-
-            to_plane(u, z, h)
-
-    def spread_step(u, s):
-        low, high = z - s, z + s
-        for h in range(parts):
-            @pl.when(low >= 0)
-            def _():
-                up_copy(u, low, h).wait_recv()
-
-                @pl.when(z + 1 < zs)
-                def _():
-                    up_copy(u, low, h).start()
-
-                to_plane(u, low, h)
-
-            @pl.when(high < zs)
-            def _():
-                dn_copy(u, high, h).wait_recv()
-
-                @pl.when(z > 0)
-                def _():
-                    dn_copy(u, high, h).start()
-
-                to_plane(u, high, h)
+                dn_copy(u, high, h).start()
+
+            to_plane(u, high, h)
+
+    waves = parts + LAG * (zs - 2)
+
+    def spread_wave(u, w):
+        for s in reversed(range(1, zs)):
+            h = w - LAG * (s - 1)
+            if 0 <= h < parts:
+                spread_step(u, s, h)
+
+    def spread_steps(u, fillers):
+        waiting = list(fillers)
+        for w in range(waves):
+            while waiting and waiting[0][0] * waves <= w:
+                waiting.pop(0)[1]()
+            spread_wave(u, w)
+            if w + ahead < parts:
+                spread_post(u, w + ahead)
+        for _, work_of in waiting:
+            work_of()
 
     def partner_copy(u, d, h):
         ref = rowbuf.at[u, slot_of(core, lax.rem(row - d + rows, rows)), part_of(h)]
@@ -364,112 +410,155 @@
 
         lax.fori_loop(begin, end, chunk, 0)
 
-    def term(n, span, high, both):
+    def half_span(k):
+        return pl.ds(pl.multiple_of(k * (rows * wide), rows * wide), rows * wide)
+
+    def split_half(u, k):
+        def piece(i, carry):
+            j = k * rows + i
+            high, low = halves(rowbuf[u, j])
+            wsplit[k, :width, pl.ds(pl.multiple_of(i * wide, wide), wide)] = high
+            wsplit[k, width:, pl.ds(pl.multiple_of(i * wide, wide), wide)] = low
+            return carry
+
+        lax.fori_loop(0, rows, piece, 0)
+
+    def half_term(k, n):
         go = functools.partial(lax.dot_general, dimension_numbers=NN, preferred_element_type=F32)
-        one = go(both, ahi[n, span, :])
-        two = go(high, alo[n, span, :])
+        one = go(wsplit[k], ahi[n, half_span(k), :])
+        two = go(wsplit[k, :width], alo[n, half_span(k), :])
         return one[:width] + one[width:] + two
 
-    def split_rows(u, j):
-        high, low = halves(rowbuf[u, j])
-        wsplit[j, :width] = high
-        wsplit[j, width:] = low
-
-    def span_of(j):
-        return pl.ds(pl.multiple_of(j * wide, wide), wide)
-
-    def product_near(u):
-        def piece(i, carry):
-            j = core * rows + i
-            split_rows(u, j)
-            for n in range(rows):
-                value = term(n, span_of(j), wsplit[j, :width], wsplit[j])
-                part[u, n] = jnp.where(i == 0, value, value + part[u, n])
+    early = min(2, rows - 1)
+
+    def product(u, rs):
+        split_half(u, core)
+
+        def near(d, carry):
+            n = lax.rem(row + d, rows)
+            part[n] = half_term(core, n)
             return carry
 
-        lax.fori_loop(0, rows, piece, 0)
-
-    def product_far(u, rs):
-        lax.fori_loop(0, rows, lambda i, c: (split_rows(u, (1 - core) * rows + i), c)[1], 0)
-
-        def target(d, carry):
+        lax.fori_loop(1, early + 1, near, 0)
+        spread_rest(u)
+        split_half(u, 1 - core)
+
+        def far(d, carry):
             n = lax.rem(row + d, rows)
-            value = part[u, n]
-            for i in range(rows):
-                j = (1 - core) * rows + i
-                value = value + term(n, span_of(j), wsplit[j, :width], wsplit[j])
-            part[u, n] = value
+            part[n] = part[n] + half_term(1 - core, n)
+            rs_copy(rs, part, d).start()
+            return carry
+
+        lax.fori_loop(1, early + 1, far, 0)
+
+        def both(d, carry):
+            n = lax.rem(row + d, rows)
+            part[n] = half_term(core, n) + half_term(1 - core, n)
 
             @pl.when(d < rows)
             def _():
-                rs_copy(rs, part.at[u], d).start()
+                rs_copy(rs, part, d).start()
 
             return carry
 
-        lax.fori_loop(1, rows + 1, target, 0)
+        lax.fori_loop(early + 1, rows + 1, both, 0)
 
     def scope(name):
         return jax.named_scope(name)
 
-    def rows_to_basis(u, inverse, other):
+    def rows_to_basis(u, inverse, other, begin, end):
         def piece(j, carry):
             value = rowbuf[u, j]
             if other is not None:
-                value = value - dot3(other, rowbuf[0, j], TN)
-            rowbuf[u, j] = dot3(inverse, value, NN)
+                value = value - dot1(other, rowbuf[0, j], TN)
+            value = dot3(inverse, value, NN)
+            rowbuf[u, j] = value
+            tall[u, pl.ds(pl.multiple_of(j * wide, wide), wide), :] = value.T * root
             return carry
 
-        lax.fori_loop(0, cols, piece, 0)
-        wide_copy(u).start()
-
-    def wide_copy(u):
-        return pltpu.make_async_copy(rowbuf.at[u], wide_ref.at[u], out_sem.at[u])
-
-    def spread_and_multiply(u, block, a, m, small):
-        with scope(f"spread_start#{u}"):
-            spread_start(u, block)
-            ar_start(a, m, small())
-        if u == 0:
-            with scope("load_rest#0"):
-                load_covariance(chunks // 2, chunks)
-        with scope(f"spread_step#{u}"):
-            for s in range(1, zs):
-                spread_step(u, s)
+        lax.fori_loop(begin, end, piece, 0)
+
+    def tall_copy(u):
+        return pltpu.make_async_copy(tall.at[u], tall_ref.at[u], out_sem.at[u])
+
+    def first_copy(d, h):
+        t = lax.rem(row + d, rows)
+        return send(
+            x_ref.at[t, part_of(h)], rsbuf.at[0, d - 1, part_of(h)], st_send.at[d - 1, h], st_recv.at[d - 1, h], (t, col)
+        )
+
+    def first_sum(h):
+        span = part_of(h)
+        total = x_ref[row, span]
+        for d in range(1, rows):
+            first_copy(d, h).wait_recv()
+            total = total + rsbuf[0, d - 1, span]
+        zbuf[0, z, span] = total
+        spread_post(0, h)
+
+    def multiply_and_sum(u):
         with scope(f"spread_half#{u}"):
-            ar_mid(a, m)
             spread_half(u)
-        with scope(f"near#{u}"):
-            product_near(u)
-        with scope(f"spread_rest#{u}"):
-            ar_late(a, m)
-            spread_rest(u)
-        with scope(f"far#{u}"):
-            product_far(u, u + 1)
+        with scope(f"product#{u}"):
+            product(u, u + 1)
 
     with scope("start#0"):
-        rs_start(0, x_ref)
-        load_covariance(0, chunks // 2)
-    with scope("rs#0"):
-        start = rs_finish(0, x_ref)
-    spread_and_multiply(0, start, 0, 1, lambda: dot(start, start, NT))
+        for h in range(parts):
+            for d in range(1, rows):
+                first_copy(d, h).start()
+        done = chunks // 4
+        load_covariance(0, done)
+    with scope("spread_steps#0"):
+        for h in range(parts):
+            first_sum(h)
+            more = chunks // 4 + (chunks - chunks // 4) * (h + 1) // (waves + 1)
+            load_covariance(done, more)
+            done = more
+            if h > 0:
+                spread_wave(0, h - 1)
+        start = zbuf[0, z]
+        ar_start(0, 1, dot(start, start, NT))
+        for w in range(parts - 1, waves):
+            more = chunks // 4 + (chunks - chunks // 4) * (w + 2) // (waves + 1)
+            load_covariance(done, more)
+            done = more
+            spread_wave(0, w)
+        for h in range(parts):
+            for d in range(1, rows):
+                first_copy(d, h).wait_send()
+        ar_mid(0, 1)
+    with scope("spread_half#0"):
+        spread_half(0)
+        ar_late(0, 1)
+    with scope("product#0"):
+        product(0, 1)
     with scope("factor#0"):
         gram = ar_finish(0, 1)
         upper0, inv0 = factor(gram, work)
         small_ref[0] = upper0
         small_ref[1] = inv0
         q0 = dot(inv0, start, NN)
+        spread_drain(0)
     with scope("rs#1"):
-        image = rs_finish(1, part.at[0])
+        image = rs_finish(1, part)
     with scope("sum#1"):
         image0 = dot(inv0, image, NN)
         ar_start(1, 1, dot(q0, image0, NT))
+        rows_to_basis(0, inv0, None, 0, cols // 2)
         ar_mid(1, 1)
+        rows_to_basis(0, inv0, None, cols // 2, cols)
         ar_late(1, 1)
+        tall_copy(0).start()
         h1 = ar_finish(1, 1)
         once = image0 - dot(h1, q0, TN)
-    spread_and_multiply(
-        1, once, 2, 2, lambda: jnp.concatenate([dot(q0, once, NT), dot(once, once, NT)], axis=0)
-    )
+    with scope("spread_start#1"):
+        spread_put(1, once)
+        for h in range(ahead):
+            spread_post(1, h)
+        ar_start(2, 2, jnp.concatenate([dot(q0, once, NT), dot(once, once, NT)], axis=0))
+    with scope("spread_steps#1"):
+        spread_steps(1, [(0.35, lambda: ar_mid(2, 2)), (0.7, lambda: ar_late(2, 2))])
+    multiply_and_sum(1)
     with scope("factor#1"):
         both = ar_finish(2, 2)
         h2, raw = both[:width], both[width:]
@@ -483,50 +572,61 @@
         q1 = dot(inv1, twice, NN)
         shift = dot(h2, image0, TN)
         stacked = jnp.concatenate([q0, q1], axis=0)
+        spread_drain(1)
     with scope("rs#2"):
-        image = rs_finish(2, part.at[1])
+        image = rs_finish(2, part)
     with scope("sum#3"):
         image1 = dot(inv1, image - shift, NN)
         ar_start(3, 2, dot(stacked, image1, NT))
-        spread_drain(0)
-        rows_to_basis(0, inv0, None)
+        rows_to_basis(1, inv1, h2, 0, cols // 2)
         ar_mid(3, 2)
+        rows_to_basis(1, inv1, h2, cols // 2, cols)
         ar_late(3, 2)
+        tall_copy(1).start()
         g1 = ar_finish(3, 2)
         once = image1 - dot(g1, stacked, TN)
     with scope("last_start#0"):
+        spread_put(2, once)
+        spread_post(2, 0)
         ar_start(4, 3, jnp.concatenate([dot(stacked, once, NT), dot(once, once, NT)], axis=0))
-        spread_start(2, once)
-    with scope("basis#1"):
-        spread_drain(1)
-        wide_copy(0).wait()
-        rows_to_basis(1, inv1, h2)
-    with scope("last_steps#0"):
-        spread_step(2, 1)
-        ar_mid(4, 3)
-        for s in range(2, zs):
-            spread_step(2, s)
-        ar_late(4, 3)
-    with scope("last_half#0"):
-        spread_half(2)
-    with scope("last_sum#0"):
+        for h in range(1, ahead):
+            spread_post(2, h)
+
+    def last_gram():
         both = ar_finish(4, 3)
-    with scope("factor#2"):
         g2, raw = both[: 2 * width], both[2 * width :]
-        gram = raw - dot(g2, g2, TN)
-        upper2, inv2 = factor(gram, work)
         small_ref[6] = g1[:width]
         small_ref[7] = g1[width:]
         small_ref[8] = g2[:width]
         small_ref[9] = g2[width:]
+        factor_begin(raw - dot(g2, g2, TN), work)
+
+    panels = width // DEEP
+
+    with scope("last_steps#0"):
+        spread_steps(2, [
+            (0.15, lambda: ar_mid(4, 3)),
+            (0.3, lambda: ar_late(4, 3)),
+            (0.45, last_gram),
+            (0.5, lambda: factor_panels(work, 0, panels // 4)),
+            (0.6, lambda: factor_panels(work, panels // 4, panels // 2)),
+            (0.7, lambda: factor_panels(work, panels // 2, panels * 3 // 4)),
+            (0.8, lambda: factor_panels(work, panels * 3 // 4, panels)),
+        ])
+    with scope("last_half#0"):
+        spread_half(2)
+    with scope("factor#2"):
+        upper2, inv2 = factor_end(work)
         small_ref[10] = upper2
         small_ref[11] = inv2
     with scope("end#0"):
         spread_rest(2)
-        wide_copy(2).start()
+        last = pltpu.make_async_copy(rowbuf.at[2], wide_ref, out_sem.at[2])
+        last.start()
         spread_drain(2)
-        wide_copy(1).wait()
-        wide_copy(2).wait()
+        tall_copy(0).wait()
+        tall_copy(1).wait()
+        last.wait()
 
 
 def main(rows, cols, x, covariance):
@@ -538,21 +638,22 @@
     uses = 3
     sums, most = 5, 3 * width // plane
     return pl.pallas_call(
-        functools.partial(main_kernel, rows, cols),
+        functools.partial(main_kernel, rows, cols, float(rows * row_count) ** 0.5),
         out_shape=(
-            jax.ShapeDtypeStruct((3, cols, width, wide), F32),
+            jax.ShapeDtypeStruct((cols, width, wide), F32),
+            jax.ShapeDtypeStruct((2, row_count, width), F32),
             jax.ShapeDtypeStruct((12, width, width), F32),
         ),
         in_specs=[pl.BlockSpec(memory_space=pltpu.VMEM), pl.BlockSpec(memory_space=pl.ANY)],
-        out_specs=(pl.BlockSpec(memory_space=pl.ANY), pl.BlockSpec(memory_space=pltpu.VMEM)),
+        out_specs=(pl.BlockSpec(memory_space=pl.ANY), pl.BlockSpec(memory_space=pl.ANY), pl.BlockSpec(memory_space=pltpu.VMEM)),
         scratch_shapes=[
             pltpu.VMEM((rows, row_count, wide), BF16),
             pltpu.VMEM((rows, row_count, wide), BF16),
             pltpu.VMEM((2, deep, col_count), F32),
             dma((2,)),
-            pltpu.VMEM((2, rows, width, wide), F32),
+            pltpu.VMEM((rows, width, wide), F32),
             pltpu.VMEM((uses, rows - 1, width, wide), F32),
-            dma((uses, rows - 1)), dma((uses, rows - 1)),
+            dma((uses, rows - 1)), dma((uses, rows - 1)), dma((rows - 1, PARTS)), dma((rows - 1, PARTS)),
             pltpu.VMEM((uses, zs, width, wide), F32),
             dma((uses, zs, PARTS)), dma((uses, zs, PARTS)), dma((uses, zs, PARTS)), dma((uses, zs, PARTS)),
             pltpu.VMEM((uses, cols, width, wide), F32),
@@ -566,64 +667,87 @@
             dma((sums, zs - 1)), dma((sums, zs - 1)),
             dma((sums, plane - 1)), dma((sums, plane - 1)),
             pltpu.VMEM((width, 2 * width), F32),
-            pltpu.VMEM((cols, 2 * width, wide), BF16),
+            pltpu.VMEM((2, 2 * width, rows * wide), BF16),
+            pltpu.VMEM((2, row_count, width), F32),
         ],
         compiler_params=pltpu.CompilerParams(collective_id=0, has_side_effects=True, vmem_limit_bytes=LIMIT),
         name="lanczos",
     )(x, covariance)
 
 
-def finish_kernel(root, wide_ref, small_ref, basis_ref, projection_ref, first_ref):
+def finish_kernel(root, wide_ref, tall_ref, small_ref, basis_ref, projection_ref, first_ref,
+                  wide_buf, tall_buf, out_buf, wide_sem, tall_sem, out_sem):
     width = small_ref.shape[1]
-    get = lambda i: small_ref[i]
-    upper0, inv0, h1, h2, upper1, inv1, g1a, g1b, g2a, g2b, upper2, inv2 = [get(i) for i in range(12)]
-    q0, q1 = wide_ref[0, 0], wide_ref[1, 0]
-    q2 = dot3(inv2, wide_ref[2, 0] - (dot3(g2a, q0, TN) + dot3(g2b, q1, TN)), NN)
-    for i, value in enumerate((q0, q1, q2)):
-        basis_ref[:, i * width : (i + 1) * width] = value.T * root
-
-    @pl.when(pl.program_id(0) == 0)
-    def _():
-        zero = jnp.zeros((width, width), F32)
-        spot = lambda i: pl.ds(i * width, width)
-        for r, c, value in (
-            (0, 0, h1 + h2), (1, 0, upper1), (2, 0, zero),
-            (0, 1, g1a + g2a), (1, 1, g1b + g2b), (2, 1, upper2),
-        ):
-            projection_ref[spot(r), spot(c)] = value
-        for r, c, value in ((0, 0, h1), (1, 0, zero), (2, 0, zero), (0, 1, g1a), (1, 1, g1b), (2, 1, zero)):
-            first_ref[spot(r), spot(c)] = value
-
-
-def finish(order, wide_blocks, small):
-    _, cols, width, wide = wide_blocks.shape
-    whole = lambda i: (0, 0)
+    cols, _, wide = wide_buf.shape
+
+    def get(j):
+        rows_of = pl.ds(pl.multiple_of(j * wide, wide), wide)
+        return (
+            pltpu.make_async_copy(wide_ref.at[j], wide_buf.at[j], wide_sem.at[j]),
+            pltpu.make_async_copy(tall_ref.at[:, rows_of], tall_buf.at[:, rows_of], tall_sem.at[j]),
+            pltpu.make_async_copy(out_buf.at[rows_of], basis_ref.at[rows_of], out_sem.at[j]),
+        )
+
+    for j in range(cols):
+        wide_in, tall_in, _ = get(j)
+        wide_in.start()
+        tall_in.start()
+    upper0, inv0, h1, h2, upper1, inv1, g1a, g1b, g2a, g2b, upper2, inv2 = [small_ref[i] for i in range(12)]
+    shift = jnp.concatenate([g2a, g2b], axis=0)
+
+    def piece(j, carry):
+        wide_in, tall_in, out = get(j)
+        wide_in.wait()
+        tall_in.wait()
+        rows_of = pl.ds(pl.multiple_of(j * wide, wide), wide)
+        q0, q1 = tall_buf[0, rows_of], tall_buf[1, rows_of]
+        twice = wide_buf[j].T * root - dot1(jnp.concatenate([q0, q1], axis=1), shift, NN)
+        out_buf[rows_of, :width] = q0
+        out_buf[rows_of, width : 2 * width] = q1
+        out_buf[rows_of, 2 * width :] = dot3(twice, inv2, NT)
+        out.start()
+        return carry
+
+    lax.fori_loop(0, cols, piece, 0)
+    zero = jnp.zeros((width, width), F32)
+    spot = lambda i: pl.ds(i * width, width)
+    for r, c, value in (
+        (0, 0, h1 + h2), (1, 0, upper1), (2, 0, zero),
+        (0, 1, g1a + g2a), (1, 1, g1b + g2b), (2, 1, upper2),
+    ):
+        projection_ref[spot(r), spot(c)] = value
+    for r, c, value in ((0, 0, h1), (1, 0, zero), (2, 0, zero), (0, 1, g1a), (1, 1, g1b), (2, 1, zero)):
+        first_ref[spot(r), spot(c)] = value
+    lax.fori_loop(0, cols, lambda j, carry: (get(j)[2].wait(), carry)[1], 0)
+
+
+def finish(order, wide_block, tall_blocks, small):
+    cols, width, wide = wide_block.shape
+    dma, vmem, anywhere = pltpu.SemaphoreType.DMA, pl.BlockSpec(memory_space=pltpu.VMEM), pl.BlockSpec(memory_space=pl.ANY)
     return pl.pallas_call(
         functools.partial(finish_kernel, float(order) ** 0.5),
-        grid=(cols,),
         out_shape=(
             jax.ShapeDtypeStruct((cols * wide, 3 * width), F32),
             jax.ShapeDtypeStruct((3 * width, 2 * width), F32),
             jax.ShapeDtypeStruct((3 * width, 2 * width), F32),
         ),
-        in_specs=[
-            pl.BlockSpec((3, 1, width, wide), lambda i: (0, i, 0, 0)),
-            pl.BlockSpec(small.shape, lambda i: (0, 0, 0)),
+        in_specs=[anywhere, anywhere, vmem],
+        out_specs=(anywhere, vmem, vmem),
+        scratch_shapes=[
+            pltpu.VMEM(wide_block.shape, F32),
+            pltpu.VMEM(tall_blocks.shape, F32),
+            pltpu.VMEM((cols * wide, 3 * width), F32),
+            dma((cols,)), dma((cols,)), dma((cols,)),
         ],
-        out_specs=(
-            pl.BlockSpec((wide, 3 * width), lambda i: (i, 0)),
-            pl.BlockSpec((3 * width, 2 * width), whole),
-            pl.BlockSpec((3 * width, 2 * width), whole),
-        ),
         compiler_params=pltpu.CompilerParams(vmem_limit_bytes=LIMIT),
         name="finish",
-    )(wide_blocks, small)
+    )(wide_block, tall_blocks, small)
 
 
 def solve(rows, cols, covariance, seed_index):
     x = gather(rows, covariance, seed_index)
-    wide_blocks, small = main(rows, cols, x, covariance)
-    return finish(rows * covariance.shape[0], wide_blocks, small)
+    wide_block, tall_blocks, small = main(rows, cols, x, covariance)
+    return finish(rows * covariance.shape[0], wide_block, tall_blocks, small)
 
 
 def solution(mesh):

time: 214 us -> 171 us (0.80)
  Pallas kernels: 210 us -> 170 us
    pallas_call x2, Pallas kernels: 204 us -> 166 us  [the longest x1 158 us: main(): pl.pallas_call(functools.partial(main_kernel, rows, cols, float(rows * ro...]
    pallas_call x1, Pallas kernels: 5.98 us -> 3.58 us  [gather(): pl.pallas_call(functools.partial(gather_kernel, rows), out_shape=jax.Shap...]
where the time goes in v3:
time: 171 us
  Pallas kernels  170 us (99%)
    pallas_call x1, Pallas kernels, main(): pl.pallas_call(functools.partial(main_kernel, rows, cols, float(rows * ro...  158 us
    pallas_call x1, Pallas kernels, finish(): pl.pallas_call(functools.partial(finish_kernel, float(order) ** 0.5), out...  8.58 us
    pallas_call x1, Pallas kernels, gather(): pl.pallas_call(functools.partial(gather_kernel, rows), out_shape=jax.Shap...  3.58 us

profile of v3, /device:TPU:7, one launch (start us, length us, event | category | flops | bytes accessed | tf_op | source)
XLA Modules:
  0.0 170.8 jit_solution(1351148354539324573)
XLA Ops:
  0.6 3.6 %gather.1.x_ref = f32[4,128,512]{2,1,0:T(8,128)} custom-call(s32[128]{0:T(128)} %index_ref.1, f32[4096,2048]{1,0:T(8,128)} %cov_ref.3), custom_call_target="tpu_custom_call" | custom-call | tf_op jit(solution)/shard_map/gather/pallas_call | solution.py:65
  4.2 157.8 %lanczos.1 = (f32[8,128,512]{2,1,0:T(8,128)}, f32[2,4096,128]{2,1,0:T(8,128)}, f32[12,128,128]{2,1,0:T(8,128)}) custom-call(f32[4,128,512]{2,1,0:T(8,128)} %gather.1.x_ref, f32[4096,2048]{1,0:T(8,128)} %cov_ref.3), custom_call_target="tpu_custom_call" | custom-call | tf_op jit(solution)/shard_map/lanczos/pallas_call | solution.py:640
  162.0 8.6 %finish.1 = (f32[4096,384]{1,0:T(8,128)}, f32[384,256]{1,0:T(8,128)}, f32[384,256]{1,0:T(8,128)}) custom-call(f32[8,128,512]{2,1,0:T(8,128)} %get-tuple-element.6.wide_ref, f32[2,4096,128]{2,1,0:T(8,128)} %get-tuple-element.7.tall_ref, f32[12,128,128]{2,1,0:T(8,128)} %get-tuple-element.8.small_ref), custom_call_target="tpu_custom_call" | custom-call | tf_op jit(solution)/shard_map/finish/pallas_call | solution.py:727

commit v4 on v3

--- a/solution.py
+++ b/solution.py
@@ -12,6 +12,7 @@
 PARTS = 8
 AHEAD = 3
 LAG = 2
+EARLY = 1
 LIMIT = 66 * 1024 * 1024 - 2 * 1024 * 1024
 
 NN = (((1,), (0,)), ((), ()))
@@ -48,13 +49,26 @@
 
     def fetch(i, keep):
         place = index_ref[i]
-        local = lax.rem(place, row_count)
-        pltpu.make_async_copy(cov_ref.at[pl.ds(local, 1), :], buf.at[pl.ds(i, 1), :], sem).start()
-        inside = jnp.where(place - local == base, 1, 0)
-        return jnp.where(tall == i, inside, keep)
+        local = place - base
+        mine = (local >= 0) & (local < row_count)
+
+        @pl.when(mine)
+        def _():
+            pltpu.make_async_copy(cov_ref.at[pl.ds(local, 1), :], buf.at[pl.ds(i, 1), :], sem).start()
+
+        return jnp.where(tall == i, jnp.where(mine, 1, 0), keep)
+
+    def drain(i, carry):
+        local = index_ref[i] - base
+
+        @pl.when((local >= 0) & (local < row_count))
+        def _():
+            pltpu.make_async_copy(cov_ref.at[pl.ds(0, 1), :], buf.at[pl.ds(i, 1), :], sem).wait()
+
+        return carry
 
     keep = lax.fori_loop(0, width, fetch, jnp.zeros((width, 1), jnp.int32), unroll=8)
-    pltpu.make_async_copy(cov_ref.at[pl.ds(0, width), :], buf, sem).wait()
+    lax.fori_loop(0, width, drain, 0, unroll=8)
     for n in range(rows):
         out_ref[n] = jnp.where(keep > 0, buf[:, n * wide : (n + 1) * wide], 0.0)
 
@@ -429,7 +443,7 @@
         two = go(wsplit[k, :width], alo[n, half_span(k), :])
         return one[:width] + one[width:] + two
 
-    early = min(2, rows - 1)
+    early = min(EARLY, rows - 1)
 
     def product(u, rs):
         split_half(u, core)
@@ -556,75 +570,112 @@
         for h in range(ahead):
             spread_post(1, h)
         ar_start(2, 2, jnp.concatenate([dot(q0, once, NT), dot(once, once, NT)], axis=0))
-    with scope("spread_steps#1"):
-        spread_steps(1, [(0.35, lambda: ar_mid(2, 2)), (0.7, lambda: ar_late(2, 2))])
-    multiply_and_sum(1)
-    with scope("factor#1"):
+
+    panels = width // DEEP
+    kept = {}
+
+    def second_gram():
         both = ar_finish(2, 2)
         h2, raw = both[:width], both[width:]
-        gram = raw - dot(h2, h2, TN)
-        upper1, inv1 = factor(gram, work)
+        factor_begin(raw - dot(h2, h2, TN), work)
         small_ref[2] = h1
         small_ref[3] = h2
+        kept["h2"] = h2
+
+    def second_factor():
+        h2 = kept["h2"]
+        upper1, inv1 = factor_end(work)
         small_ref[4] = upper1
         small_ref[5] = inv1
         twice = once - dot(h2, q0, TN)
-        q1 = dot(inv1, twice, NN)
-        shift = dot(h2, image0, TN)
-        stacked = jnp.concatenate([q0, q1], axis=0)
+        kept["inv1"] = inv1
+        kept["stacked"] = jnp.concatenate([q0, dot(inv1, twice, NN)], axis=0)
+        kept["shift"] = dot(h2, image0, TN)
+
+    with scope("spread_steps#1"):
+        spread_steps(1, [
+            (0.35, lambda: ar_mid(2, 2)), (0.7, lambda: ar_late(2, 2)),
+        ])
+    multiply_and_sum(1)
+    with scope("factor#1"):
+        second_gram()
+        factor_panels(work, 0, panels)
+        second_factor()
         spread_drain(1)
+        h2, inv1, stacked = kept["h2"], kept["inv1"], kept["stacked"]
     with scope("rs#2"):
         image = rs_finish(2, part)
-    with scope("sum#3"):
-        image1 = dot(inv1, image - shift, NN)
+    with scope("last_start#0"):
+        image1 = dot(inv1, image - kept["shift"], NN)
+        spread_put(2, image1)
+        spread_post(2, 0)
         ar_start(3, 2, dot(stacked, image1, NT))
-        rows_to_basis(1, inv1, h2, 0, cols // 2)
-        ar_mid(3, 2)
-        rows_to_basis(1, inv1, h2, cols // 2, cols)
-        ar_late(3, 2)
-        tall_copy(1).start()
+        for h in range(1, ahead):
+            spread_post(2, h)
+
+    def basis_part(i):
+        return lambda: rows_to_basis(1, inv1, h2, cols * i // 4, cols * (i + 1) // 4)
+
+    def last_project():
         g1 = ar_finish(3, 2)
         once = image1 - dot(g1, stacked, TN)
-    with scope("last_start#0"):
-        spread_put(2, once)
-        spread_post(2, 0)
         ar_start(4, 3, jnp.concatenate([dot(stacked, once, NT), dot(once, once, NT)], axis=0))
-        for h in range(1, ahead):
-            spread_post(2, h)
+        small_ref[6] = g1[:width]
+        small_ref[7] = g1[width:]
+        kept["g1"] = g1
+
+    def fold_spot(j, b):
+        return pl.ds(pl.multiple_of(j * wide + b * width, width), width)
+
+    def fold_part(i):
+        def piece(j, carry):
+            value = dot3(kept["g1"], jnp.concatenate([rowbuf[0, j], rowbuf[1, j]], axis=0), TN)
+            for b in range(wide // width):
+                tall[0, fold_spot(j, b), :] = value[:, b * width : (b + 1) * width]
+            return carry
+
+        return lambda: lax.fori_loop(cols * i // 4, cols * (i + 1) // 4, piece, 0)
+
+    def fold():
+        def piece(j, carry):
+            for b in range(wide // width):
+                span = slice(b * width, (b + 1) * width)
+                rowbuf[2, j, :, span] = rowbuf[2, j, :, span] - tall[0, fold_spot(j, b), :]
+            return carry
+
+        lax.fori_loop(0, cols, piece, 0)
 
     def last_gram():
         both = ar_finish(4, 3)
         g2, raw = both[: 2 * width], both[2 * width :]
-        small_ref[6] = g1[:width]
-        small_ref[7] = g1[width:]
         small_ref[8] = g2[:width]
         small_ref[9] = g2[width:]
         factor_begin(raw - dot(g2, g2, TN), work)
 
-    panels = width // DEEP
-
     with scope("last_steps#0"):
         spread_steps(2, [
-            (0.15, lambda: ar_mid(4, 3)),
-            (0.3, lambda: ar_late(4, 3)),
-            (0.45, last_gram),
-            (0.5, lambda: factor_panels(work, 0, panels // 4)),
-            (0.6, lambda: factor_panels(work, panels // 4, panels // 2)),
-            (0.7, lambda: factor_panels(work, panels // 2, panels * 3 // 4)),
-            (0.8, lambda: factor_panels(work, panels * 3 // 4, panels)),
+            (0.0, basis_part(0)), (0.1, lambda: ar_mid(3, 2)), (0.1, basis_part(1)), (0.25, lambda: ar_late(3, 2)),
+            (0.25, basis_part(2)), (0.4, last_project), (0.4, basis_part(3)), (0.4, lambda: tall_copy(1).start()),
+            (0.5, lambda: tall_copy(0).wait()), (0.5, fold_part(0)),
+            (0.6, lambda: ar_mid(4, 3)), (0.6, fold_part(1)), (0.7, fold_part(2)), (0.8, lambda: ar_late(4, 3)),
+            (0.85, fold_part(3)),
         ])
+    with scope("last_gram#0"):
+        last_gram()
+        factor_panels(work, 0, panels // 2)
     with scope("last_half#0"):
         spread_half(2)
     with scope("factor#2"):
+        factor_panels(work, panels // 2, panels)
         upper2, inv2 = factor_end(work)
         small_ref[10] = upper2
         small_ref[11] = inv2
     with scope("end#0"):
         spread_rest(2)
+        spread_drain(2)
+        fold()
         last = pltpu.make_async_copy(rowbuf.at[2], wide_ref, out_sem.at[2])
         last.start()
-        spread_drain(2)
-        tall_copy(0).wait()
         tall_copy(1).wait()
         last.wait()
 

time: 171 us -> 167 us (0.977)
  Pallas kernels: 170 us -> 165 us
    pallas_call x1, Pallas kernels: 158 us -> 153 us  [main(): pl.pallas_call(functools.partial(main_kernel, rows, cols, float(rows * ro...]
where the time goes in v4:
time: 167 us; the launch traced here: 166 us
  Pallas kernels  165 us (99%)
    pallas_call x1, Pallas kernels, main(): pl.pallas_call(functools.partial(main_kernel, rows, cols, float(rows * ro...  153 us
    pallas_call x1, Pallas kernels, finish(): pl.pallas_call(functools.partial(finish_kernel, float(order) ** 0.5), out...  8.57 us
    pallas_call x1, Pallas kernels, gather(): pl.pallas_call(functools.partial(gather_kernel, rows), out_shape=jax.Shap...  3.59 us

profile of v4, /device:TPU:7, one launch (start us, length us, event | category | flops | bytes accessed | tf_op | source)
XLA Modules:
  0.0 165.6 jit_solution(17849653382160039785)
XLA Ops:
  0.6 3.6 %gather.1.x_ref = f32[4,128,512]{2,1,0:T(8,128)} custom-call(s32[128]{0:T(128)} %index_ref.1, f32[4096,2048]{1,0:T(8,128)} %cov_ref.3), custom_call_target="tpu_custom_call" | custom-call | tf_op jit(solution)/shard_map/gather/pallas_call | solution.py:79
  4.2 152.6 %lanczos.1 = (f32[8,128,512]{2,1,0:T(8,128)}, f32[2,4096,128]{2,1,0:T(8,128)}, f32[12,128,128]{2,1,0:T(8,128)}) custom-call(f32[4,128,512]{2,1,0:T(8,128)} %gather.1.x_ref, f32[4096,2048]{1,0:T(8,128)} %cov_ref.3), custom_call_target="tpu_custom_call" | custom-call | tf_op jit(solution)/shard_map/lanczos/pallas_call | solution.py:691
  156.8 8.6 %finish.1 = (f32[4096,384]{1,0:T(8,128)}, f32[384,256]{1,0:T(8,128)}, f32[384,256]{1,0:T(8,128)}) custom-call(f32[8,128,512]{2,1,0:T(8,128)} %get-tuple-element.6.wide_ref, f32[2,4096,128]{2,1,0:T(8,128)} %get-tuple-element.7.tall_ref, f32[12,128,128]{2,1,0:T(8,128)} %get-tuple-element.8.small_ref), custom_call_target="tpu_custom_call" | custom-call | tf_op jit(solution)/shard_map/finish/pallas_call | solution.py:778

commit v5 on v4

--- a/solution.py
+++ b/solution.py
@@ -654,11 +654,21 @@
 
     with scope("last_steps#0"):
         spread_steps(2, [
-            (0.0, basis_part(0)), (0.1, lambda: ar_mid(3, 2)), (0.1, basis_part(1)), (0.25, lambda: ar_late(3, 2)),
-            (0.25, basis_part(2)), (0.4, last_project), (0.4, basis_part(3)), (0.4, lambda: tall_copy(1).start()),
-            (0.5, lambda: tall_copy(0).wait()), (0.5, fold_part(0)),
-            (0.6, lambda: ar_mid(4, 3)), (0.6, fold_part(1)), (0.7, fold_part(2)), (0.8, lambda: ar_late(4, 3)),
-            (0.85, fold_part(3)),
+            (0.0, basis_part(0)),
+            (0.1, lambda: ar_mid(3, 2)),
+            (0.1, basis_part(1)),
+            (0.25, lambda: ar_late(3, 2)),
+            (0.25, basis_part(2)),
+            (0.4, last_project),
+            (0.41, basis_part(3)),
+            (0.41, lambda: tall_copy(1).start()),
+            (0.5, lambda: ar_mid(4, 3)),
+            (0.5, lambda: tall_copy(0).wait()),
+            (0.5, fold_part(0)),
+            (0.6, fold_part(1)),
+            (0.66, lambda: ar_late(4, 3)),
+            (0.66, fold_part(2)),
+            (0.8, fold_part(3)),
         ])
     with scope("last_gram#0"):
         last_gram()

time: 167 us -> 167 us (level)
  no operation moved by 1% of the time
where the time goes in v5:
time: 167 us; the launch traced here: 166 us
  Pallas kernels  165 us (99%)
    pallas_call x1, Pallas kernels, main(): pl.pallas_call(functools.partial(main_kernel, rows, cols, float(rows * ro...  153 us
    pallas_call x1, Pallas kernels, finish(): pl.pallas_call(functools.partial(finish_kernel, float(order) ** 0.5), out...  8.58 us
    pallas_call x1, Pallas kernels, gather(): pl.pallas_call(functools.partial(gather_kernel, rows), out_shape=jax.Shap...  3.59 us

profile of v5, /device:TPU:7, one launch (start us, length us, event | category | flops | bytes accessed | tf_op | source)
XLA Modules:
  0.0 166.2 jit_solution(8606232107419609899)
XLA Ops:
  0.6 3.6 %gather.1.x_ref = f32[4,128,512]{2,1,0:T(8,128)} custom-call(s32[128]{0:T(128)} %index_ref.1, f32[4096,2048]{1,0:T(8,128)} %cov_ref.3), custom_call_target="tpu_custom_call" | custom-call | tf_op jit(solution)/shard_map/gather/pallas_call | solution.py:79
  4.2 153.2 %lanczos.1 = (f32[8,128,512]{2,1,0:T(8,128)}, f32[2,4096,128]{2,1,0:T(8,128)}, f32[12,128,128]{2,1,0:T(8,128)}) custom-call(f32[4,128,512]{2,1,0:T(8,128)} %gather.1.x_ref, f32[4096,2048]{1,0:T(8,128)} %cov_ref.3), custom_call_target="tpu_custom_call" | custom-call | tf_op jit(solution)/shard_map/lanczos/pallas_call | solution.py:701
  157.4 8.6 %finish.1 = (f32[4096,384]{1,0:T(8,128)}, f32[384,256]{1,0:T(8,128)}, f32[384,256]{1,0:T(8,128)}) custom-call(f32[8,128,512]{2,1,0:T(8,128)} %get-tuple-element.6.wide_ref, f32[2,4096,128]{2,1,0:T(8,128)} %get-tuple-element.7.tall_ref, f32[12,128,128]{2,1,0:T(8,128)} %get-tuple-element.8.small_ref), custom_call_target="tpu_custom_call" | custom-call | tf_op jit(solution)/shard_map/finish/pallas_call | solution.py:788
